TPU v7x, 128 devices: a whole 4x4x4 slice. The times are simulated.
128 devices in a mesh: rep: 1, dp: 128 (over x, y, z, core).
Axes of the slice: x: 4, y: 4, z: 4, core: 2. Of those that a mesh axis runs over, the one named last changes fastest.
Arguments:
- g_w_gate: bfloat16 [128, 2, 512, 8192], P(('rep', 'dp'))
- g_w_up: bfloat16 [128, 2, 512, 8192], P(('rep', 'dp'))
- g_w_down: bfloat16 [128, 2, 8192, 512], P(('rep', 'dp'))
- w_gate: bfloat16 [2, 512, 8192], replicated
- w_up: bfloat16 [2, 512, 8192], replicated
- w_down: bfloat16 [2, 8192, 512], replicated
- m_w_gate: float32 [2, 512, 8192], P(None, 'dp')
- m_w_up: float32 [2, 512, 8192], P(None, 'dp')
- m_w_down: float32 [2, 8192, 512], P(None, 'dp')
- v_w_gate: float32 [2, 512, 8192], P(None, 'dp')
- v_w_up: float32 [2, 512, 8192], P(None, 'dp')
- v_w_down: float32 [2, 8192, 512], P(None, 'dp')
Outputs:
- output 1: bfloat16 [2, 512, 8192], P('rep')
- output 2: bfloat16 [2, 512, 8192], P('rep')
- output 3: bfloat16 [2, 8192, 512], P('rep')
- output 4: float32 [2, 512, 8192], P('rep', 'dp')
- output 5: float32 [2, 512, 8192], P('rep', 'dp')
- output 6: float32 [2, 8192, 512], P('rep', 'dp')
- output 7: float32 [2, 512, 8192], P('rep', 'dp')
- output 8: float32 [2, 512, 8192], P('rep', 'dp')
- output 9: float32 [2, 8192, 512], P('rep', 'dp')
All inputs are finite; a program needn't handle non-finite values.
Results may differ from a plain program's by a relative error of at most 0.022.
Values are sent between devices in bfloat16 or wider.
A program may use at most 1.5 GiB of HBM per device.

v0:
```python
import jax
import jax.numpy as jnp
from jax import lax
from jax.sharding import PartitionSpec as P


def adamw(w, m, v, g):
    m = 0.9 * m + 0.1 * g
    v = 0.95 * v + 0.05 * g * g
    step = m * lax.rsqrt(v + 1e-8) + 0.1 * w
    return (w - 0.02 * step).astype(jnp.bfloat16), m, v


def clipped(gradients, sum_of_squares, count):
    factor = jnp.minimum(1.0, 0.5 * lax.rsqrt(sum_of_squares / count + 1e-30))
    return [g * factor for g in gradients]


def solution(mesh):
    def step(*arrays):
        terms, weights, m, v = (arrays[i : i + 3] for i in (0, 3, 6, 9))
        gradients = [lax.psum_scatter(t[0], "dp", scatter_dimension=1, tiled=True).astype(jnp.float32) for t in terms]
        squares = lax.psum(sum(jnp.sum(g * g) for g in gradients), "dp")
        gradients = clipped(gradients, squares, lax.psum(1, "dp") * sum(g.size for g in gradients))
        me = lax.axis_index("dp")
        own = [lax.dynamic_slice_in_dim(w, me * one.shape[1], one.shape[1], 1).astype(jnp.float32) for w, one in zip(weights, m, strict=True)]
        new = [adamw(w, m, v, g) for w, m, v, g in zip(own, m, v, gradients, strict=True)]
        whole = [lax.all_gather(one[0], "dp", axis=1, tiled=True) for one in new]
        return (*whole, *(one[1] for one in new), *(one[2] for one in new))

    all_of, cut = P(None, None, None), P(None, "dp", None)
    return jax.shard_map(
        step,
        mesh=mesh,
        in_specs=(P(("rep", "dp"), None, None, None),) * 3 + (all_of,) * 3 + (cut,) * 6,
        out_specs=(P("rep", None, None),) * 3 + (P("rep", "dp", None),) * 6,
        check_vma=False,
    )
```

profile of v0, /device:TPU:1, one launch (start us, length us, event | category | flops | bytes accessed | tf_op | source)
XLA Modules:
  0.0 1305.3 jit_solution(9096644659200403051)
XLA Ops:
  7.2 0.0 all-reduce.5.cloned.1.call-start
  7.2 0.7 all-reduce.5.cloned.1.call-update
  8.0 0.0 reduce-scatter.4.cloned.1.call-start
  8.0 0.7 reduce-scatter.4.cloned.1.call-update
  8.7 0.0 all-gather.4.cloned.1.call-start
  8.8 293.1 %all-reduce.5.cloned.1.call-done = (bf16[2,512,8192]{2,1,0:T(8,128)(2,1)}, bf16[2,512,8192]{2,1,0:T(8,128)(2,1)}) async-done(((bf16[2,512,8192]{2,1,0:T(8,128)(2,1)}, bf16[2,512,8192]{2,1,0:T(8,128)(2,1)}), (bf16[2,512,8192]{2,1,0:T(8,128)(2,1)}, bf16[2,512,8192]{2,1,0:T(8,128)(2,1)})) %all-reduce.5.cloned.1.call-update) | async-done | bytes 33554448
  301.9 1.8 fusion.9
  305.0 662.7 %reduce-scatter.4.cloned.1.call-done = bf16[2,64,512]{2,1,0:T(8,128)(2,1)} async-done(((bf16[2,8192,512]{2,1,0:T(8,128)(2,1)}), bf16[2,64,512]{2,1,0:T(8,128)(2,1)}) %reduce-scatter.4.cloned.1.call-update) | async-done | bytes 131088 | tf_op jit(solution)/shard_map/reduce_scatter | solution.py:22
  967.7 1.6 fusion.11
  969.9 69.3 %psum.7 = f32[]{:T(128)} all-reduce(f32[]{:T(128)S(6)} %add.65), channel_id=1, replica_groups=mesh['rep'=1,'dp'=128] {'dp'}, use_global_device_ids=true, to_apply=%region_6.0 | all-reduce | flops 1 | bytes 8 | tf_op jit(solution)/shard_map/psum | solution.py:23
  1040.0 2.2 fusion.8
  1042.2 0.8 copy.21
  1043.0 0.0 all-gather.6.cloned.1.call-start
  1043.0 2.2 fusion.14
  1045.2 0.8 copy.22
  1046.0 0.0 all-gather.6.cloned.1.call-update
  1046.1 0.0 all-gather.8.cloned.1.call-start
  1046.1 1.9 fusion.17
  1048.0 71.5 %all-gather.4.cloned.1.call-done = bf16[2,512,8192]{2,0,1:T(2,128)(2,1)} async-done(((bf16[2,4,8192]{2,0,1:T(2,128)(2,1)}), bf16[2,512,8192]{2,0,1:T(2,128)(2,1)}) %all-gather.4.cloned.1.call-update) | async-done | bytes 16777232 | tf_op jit(solution)/shard_map/all_gather | solution.py:28
  1119.6 18.5 %copy.23 = bf16[2,512,8192]{2,1,0:T(8,128)(2,1)} copy(bf16[2,512,8192]{2,0,1:T(2,128)(2,1)} %all-gather.4.cloned.1.call-done) | data formatting | bytes 33554432
  1138.1 64.2 %all-gather.6.cloned.1.call-done = bf16[2,512,8192]{2,0,1:T(2,128)(2,1)} async-done(((bf16[2,4,8192]{2,0,1:T(2,128)(2,1)}), bf16[2,512,8192]{2,0,1:T(2,128)(2,1)}) %all-gather.6.cloned.1.call-update) | async-done | bytes 16777232 | tf_op jit(solution)/shard_map/all_gather | solution.py:28
  1202.3 18.5 %copy.24 = bf16[2,512,8192]{2,1,0:T(8,128)(2,1)} copy(bf16[2,512,8192]{2,0,1:T(2,128)(2,1)} %all-gather.6.cloned.1.call-done) | data formatting | bytes 33554432
  1220.8 64.2 %all-gather.8.cloned.1.call-done = bf16[2,8192,512]{2,1,0:T(8,128)(2,1)} async-done(((bf16[2,64,512]{2,1,0:T(8,128)(2,1)}), bf16[2,8192,512]{2,1,0:T(8,128)(2,1)}) %all-gather.8.cloned.1.call-update) | async-done | bytes 16777232 | tf_op jit(solution)/shard_map/all_gather | solution.py:28
  1285.0 13.8 %copy.34 = bf16[2,8192,512]{2,1,0:T(8,128)(2,1)} copy(bf16[2,8192,512]{2,1,0:T(8,128)(2,1)} %all-gather.8.cloned.1.call-done) | data formatting | bytes 33554432
  (14 shorter events, 0.1 us)
Async XLA Ops:
  7.2 294.7 %all-reduce.5.cloned.1.call-start = ((), (), s32[]{:S(2)}) async-start(), calls=%async_computation.5 | async-start | bytes 67108864
  7.9 1032.0 %copy-start.2 = (f32[2,4,8192]{2,1,0:T(4,128)S(1)}, f32[2,4,8192]{2,1,0:T(4,128)}, u32[]{:S(2)}) copy-start(f32[2,4,8192]{2,1,0:T(4,128)} %param.21) | copy-start | bytes 786436
  7.9 1032.0 %copy-start.3 = (f32[2,4,8192]{2,1,0:T(4,128)S(1)}, f32[2,4,8192]{2,1,0:T(4,128)}, u32[]{:S(2)}) copy-start(f32[2,4,8192]{2,1,0:T(4,128)} %param.18) | copy-start | bytes 786436
  7.9 1035.1 %copy-start.4 = (f32[2,4,8192]{2,1,0:T(4,128)S(1)}, f32[2,4,8192]{2,1,0:T(4,128)}, u32[]{:S(2)}) copy-start(f32[2,4,8192]{2,1,0:T(4,128)} %param.22) | copy-start | bytes 786436
  7.9 1035.1 %copy-start.5 = (f32[2,4,8192]{2,1,0:T(4,128)S(1)}, f32[2,4,8192]{2,1,0:T(4,128)}, u32[]{:S(2)}) copy-start(f32[2,4,8192]{2,1,0:T(4,128)} %param.19) | copy-start | bytes 786436
  8.0 1038.2 %copy-start = (f32[2,64,512]{2,1,0:T(8,128)S(1)}, f32[2,64,512]{2,1,0:T(8,128)}, u32[]{:S(2)}) copy-start(f32[2,64,512]{2,1,0:T(8,128)} %param.23) | copy-start | bytes 786436
  8.0 1038.2 %copy-start.1 = (f32[2,64,512]{2,1,0:T(8,128)S(1)}, f32[2,64,512]{2,1,0:T(8,128)}, u32[]{:S(2)}) copy-start(f32[2,64,512]{2,1,0:T(8,128)} %param.20) | copy-start | bytes 786436
  8.0 959.7 %reduce-scatter.4.cloned.1.call-start = ((), (), s32[]{:S(2)}) async-start(), calls=%async_computation.1 | async-start | bytes 16908288 | tf_op jit(solution)/shard_map/reduce_scatter | solution.py:22
  8.7 1110.8 %all-gather.4.cloned.1.call-start = ((), (), s32[]{:S(2)}) async-start(), calls=%async_computation.2 | async-start | bytes 16908288 | tf_op jit(solution)/shard_map/all_gather | solution.py:28
  1043.0 159.3 %all-gather.6.cloned.1.call-start = ((), (), s32[]{:S(2)}) async-start(), calls=%async_computation.3 | async-start | bytes 16908288 | tf_op jit(solution)/shard_map/all_gather | solution.py:28
  1046.1 238.9 %all-gather.8.cloned.1.call-start = ((), (), s32[]{:S(2)}) async-start(), calls=%async_computation.4 | async-start | bytes 16908288 | tf_op jit(solution)/shard_map/all_gather | solution.py:28
Sparse Core Ops, SparseCore 0:
  13.9 287.9 all-reduce.4
  304.3 663.4 reduce-scatter.3
  1043.1 76.4 all-gather.3
  1123.1 79.1 all-gather.5
  1205.2 79.7 all-gather.7
where the time goes:
time: 1310 us
  waiting for transfers between devices  1160 us (89%)
  blocking collectives  69.3 us (5%)
  local copies, waits for them, and re-layouts  52.5 us (4%)
  between operations  16.5 us (1%)
    reduce_scatter x1, waiting for transfers between devices, step(): lax.psum_scatter(t[0], 'dp', scatter_dimension=1, tiled=True)  663 us
    unnamed x6, waiting for transfers between devices  295 us
    all_gather x3, waiting for transfers between devices, step(): whole = [lax.all_gather(one[0], 'dp', axis=1, tiled=True) for one in new]  200 us
    psum x1, blocking collectives, step(): squares = lax.psum(sum((jnp.sum(g * g) for g in gradients)), 'dp')  69.3 us
    unnamed x15, local copies, waits for them, and re-layouts  50.9 us
  transfers between devices with their start and end apart: 5, of which 5 were waited for; matrix products, arithmetic and copies ran while one was open for 3% of the time, Pallas kernels for 0%

commit v1 on v0

v1 whole, which is shorter than its diff:
```python
import functools

import jax
import jax.numpy as jnp
from jax import lax
from jax.experimental import pallas as pl
from jax.experimental.pallas import tpu as pltpu
from jax.sharding import PartitionSpec as P

N = 4
DEVICES = 2 * N**3
ORDERS = ((0, 1, 2), (1, 2, 0), (2, 0, 1))
COLORS = tuple((which, layer) for which in range(3) for layer in range(2))
F32, BF16 = jnp.float32, jnp.bfloat16


def place():
    me = lax.axis_index("dp")
    chip = me // 2
    return lax.rem(me, 2), (chip // (N * N), lax.rem(chip // N, N), lax.rem(chip, N))


def device(core, chip):
    return {"dp": ((chip[0] * N + chip[1]) * N + chip[2]) * 2 + core}


def moved(chip, axis, by):
    return tuple(lax.rem(c + by + N, N) if a == axis else c for a, c in enumerate(chip))


def along(color, chip):
    which, layer = color
    axes = ORDERS[which]
    return axes, 1 - 2 * layer, tuple(chip[a] for a in axes)


def back(c, s, by):
    return lax.rem(c - s * by + N, N)


def block(ref, color, abc, tiles):
    axes = ORDERS[color[0]]
    where = [slice(None)] * 3
    for a, c in zip(axes, abc, strict=True):
        if c is not None:
            where[a] = c
    return ref.at[(color[1], *where, tiles)]


def send(src, dst, send_sem, recv_sem, to):
    copy = pltpu.make_async_remote_copy(
        src_ref=src, dst_ref=dst, send_sem=send_sem, recv_sem=recv_sem, device_id=to, device_id_type=pl.DeviceIdType.MESH
    )
    copy.start()
    return copy


def arrived(ref, sem):
    pltpu.make_async_copy(ref, ref, sem).wait()


def meet(peers):
    barrier = pltpu.get_barrier_semaphore()
    for peer in peers:
        pl.semaphore_signal(barrier, inc=1, device_id=peer, device_id_type=pl.DeviceIdType.MESH)
    pl.semaphore_wait(barrier, len(peers))


def add_up(out, ins, step):
    @pl.loop(0, out.shape[0] // step)
    def _(n):
        at = pl.ds(n * step, step)
        total = ins[0][at].astype(F32)
        for one in ins[1:]:
            total = total + one[at].astype(F32)
        out[at] = total.astype(out.dtype)


def scatter_kernel(
    g0, g1, g2, w0, w1, w2, m_wide, m_tall, v_wide, v_tall,
    w_out, g_wide, g_tall, factor_out,
    own, par, r1, r2, r3, g_send, w_chip, w_chip_tall, w_rows, w_got, norm, norm_got, mom,
    own_sem, par_send, par_recv, send1, recv1, send2, recv2, send3, recv3,
    norm_send, norm_recv, swap_send, swap_recv, back_send, back_recv, load_sem,
):
    g, w = (g0, g1, g2), (w0, w1, w2)
    core, chip = place()
    half = w_out.shape[1]
    step = min(8, half)
    mine, theirs = pl.ds(core * half, half), pl.ds((1 - core) * half, half)
    partner = device(1 - core, chip)
    meet([partner] + [device(core, moved(chip, axis, by)) for axis in range(3) for by in range(1, N)])

    def targets(color, t, k):
        axes, s, (a, b, c) = along(color, chip)
        return back(a, s, t + 1), back(b, s, k + 1), None

    def own_copy(n, t, k):
        return pltpu.make_async_copy(block(g[COLORS[n][0]], COLORS[n], targets(COLORS[n], t, k), mine), own.at[k, n], own_sem.at[k, n])

    def push(n, t, k):
        own_copy(n, t, k).start()
        src = block(g[COLORS[n][0]], COLORS[n], targets(COLORS[n], t, k), theirs)
        send(src, par.at[n, t, k], par_send.at[n, t, k], par_recv.at[n, t, k], partner)

    @pl.loop(0, N)
    def _(k):
        for n in range(6):
            push(n, 0, k)

    loads = []
    for n, (which, layer) in enumerate(COLORS):
        if which < 2:
            loads.append((block(w[which], COLORS[n], along(COLORS[n], chip)[2], slice(None)), w_chip.at[n]))
        else:
            loads.append((block(w[which], COLORS[n], along(COLORS[n], chip)[2], mine), w_chip_tall.at[layer]))
    loads = [pltpu.make_async_copy(src, dst, load_sem.at[i]) for i, (src, dst) in enumerate(loads)]
    for load in loads:
        load.start()

    def flat(ref):
        return [ref.at[q] for q in range(N)]

    def ready(n, t, k):
        own_copy(n, t, k).wait()
        arrived(par.at[n, t, k], par_recv.at[n, t, k])

    def along_a(n, t, k, first):
        axes, s, _ = along(COLORS[n], chip)
        ready(n, t, k)
        ins = [own.at[k, n], par.at[n, t, k]]
        if not first:
            arrived(r1.at[n, t - 1, k], recv1.at[n, t - 1, k])
            ins.append(r1.at[n, t - 1, k])

        @pl.loop(0, N)
        def _(q):
            add_up(par.at[n, t, k, q], [one.at[q] for one in ins], step)

        send(par.at[n, t, k], r1.at[n, t, k], send1.at[n, t, k], recv1.at[n, t, k], device(core, moved(chip, axes[0], s)))
        push(n, t + 1, k)

    @pl.loop(0, N)
    def _(k):
        for n in range(6):
            along_a(n, 0, k, True)

    @pl.loop(0, 2 * N)
    def _(i):
        for n in range(6):
            along_a(n, 1 + i // N, lax.rem(i, N), False)

    def along_b(n, k, j, first):
        axes, s, (a, b, c) = along(COLORS[n], chip)
        to = back(c, s, j + 1)
        ins = [own.at[k, n, to], par.at[n, N - 1, k, to], r1.at[n, N - 2, k, to]]
        if not first:
            arrived(r2.at[n, k - 1, to], recv2.at[n, k - 1, j])
            ins.append(r2.at[n, k - 1, to])
        out = par.at[n, N - 1, k, to]
        add_up(out, ins, step)
        send(out, r2.at[n, k, to], send2.at[n, k, j], recv2.at[n, k, j], device(core, moved(chip, axes[1], s)))

    def phase_b(k, first):
        for n in range(6):
            ready(n, N - 1, k)
            arrived(r1.at[n, N - 2, k], recv1.at[n, N - 2, k])

        @pl.loop(0, N)
        def _(j):
            for n in range(6):
                along_b(n, k, j, first)

    phase_b(0, True)

    @pl.loop(1, N - 1)
    def _(k):
        phase_b(k, False)

    def parts_c(n, j, first):
        axes, s, (a, b, c) = along(COLORS[n], chip)
        k = N - 1
        to = back(c, s, j + 1)
        arrived(r2.at[n, k - 1, to], recv2.at[n, k - 1, j])
        ins = [own.at[k, n, to], par.at[n, N - 1, k, to], r1.at[n, N - 2, k, to], r2.at[n, k - 1, to]]
        if not first:
            arrived(r3.at[n, j - 1], recv3.at[n, j - 1])
            ins.append(r3.at[n, j - 1])
        return par.at[n, N - 1, k, to], ins

    def along_c(n, j, first):
        axes, s, _ = along(COLORS[n], chip)
        out, ins = parts_c(n, j, first)
        add_up(out, ins, step)
        send(out, r3.at[n, j], send3.at[n, j], recv3.at[n, j], device(core, moved(chip, axes[2], s)))

    for n in range(6):
        ready(n, N - 1, N - 1)
        arrived(r1.at[n, N - 2, N - 1], recv1.at[n, N - 2, N - 1])
        along_c(n, 0, True)

    @pl.loop(1, N - 1)
    def _(j):
        for n in range(6):
            along_c(n, j, False)

    norm[0] = jnp.zeros(norm.shape[1:], F32)
    for n, (which, layer) in enumerate(COLORS):
        _, ins = parts_c(n, N - 1, False)

        @pl.loop(0, half // step, init_carry=jnp.zeros(norm.shape[1:], F32))
        def squares(i, so_far, ins=ins, which=which, layer=layer, n=n):
            at = pl.ds(i * step, step)
            total = ins[0][at].astype(F32)
            for one in ins[1:]:
                total = total + one[at].astype(F32)
            rounded = total.astype(BF16)
            total = rounded.astype(F32)
            if which < 2:
                low, high = total[:, :4], total[:, 4:]
                g_wide[n, pl.ds(core * half + i * step, step)] = jnp.where(core == 0, low, high).astype(BF16)
                g_send[n, at] = jnp.where(core == 0, high, low).astype(BF16)
            else:
                g_tall[layer, at] = rounded
            return so_far + jnp.sum(total * total, axis=0)

        norm[0] += squares
        if which < 2:
            send(g_send.at[n], g_wide.at[n, mine], swap_send.at[n], swap_recv.at[n], partner)

    send(norm.at[0], norm_got.at[0, 0], norm_send.at[0, 0], norm_recv.at[0, 0], partner)
    arrived(norm_got.at[0, 0], norm_recv.at[0, 0])
    norm[1] = norm[0] + norm_got[0, 0]
    for axis in range(3):
        for d in range(1, N):
            send(
                norm.at[1 + axis], norm_got.at[1 + axis, d - 1], norm_send.at[1 + axis, d - 1], norm_recv.at[1 + axis, d - 1],
                device(core, moved(chip, axis, d)),
            )
        total = norm[1 + axis]
        for d in range(1, N):
            arrived(norm_got.at[1 + axis, d - 1], norm_recv.at[1 + axis, d - 1])
            total = total + norm_got[1 + axis, d - 1]
        norm[2 + axis] = total
    count = 6 * N**3 * 2 * half * 8 * 128
    everything = jnp.sum(norm[4], keepdims=True)
    factor = jnp.minimum(1.0, 0.5 * lax.rsqrt(everything / count + 1e-30))
    factor_out[...] = jnp.broadcast_to(factor, factor_out.shape)

    for load in loads:
        load.wait()
    for n in range(4):
        arrived(g_wide.at[n, theirs], swap_recv.at[n])

    def new_weight(old, m, v, grad):
        m = 0.9 * m + 0.1 * grad
        v = 0.95 * v + 0.05 * grad * grad
        return (old - 0.02 * (m * lax.rsqrt(v + 1e-8) + 0.1 * old)).astype(BF16)

    for n in range(4):

        @pl.loop(0, 2 * half // step)
        def _(i, n=n):
            at = pl.ds(i * step, step)
            old = w_chip[n, at].astype(F32)
            old = jnp.where(core == 0, old[:, :4], old[:, 4:])
            scale = jnp.broadcast_to(factor[:, :, None], old.shape)
            w_rows[n, at] = new_weight(old, m_wide[n, at], v_wide[n, at], g_wide[n, at].astype(F32) * scale)

        send(w_rows.at[n, theirs], w_got.at[n], back_send.at[n], back_recv.at[n], partner)

    for layer in range(2):

        @pl.loop(0, half // step)
        def _(i, layer=layer):
            at = pl.ds(i * step, step)
            old = w_chip_tall[layer, at].astype(F32)
            scale = jnp.broadcast_to(factor[:, :, None], old.shape)
            w_out[4 + layer, at] = new_weight(old, m_tall[layer, at], v_tall[layer, at], g_tall[layer, at].astype(F32) * scale)

    for n in range(4):
        arrived(w_got.at[n], back_recv.at[n])

        @pl.loop(0, half // step)
        def _(i, n=n):
            at = pl.ds(i * step, step)
            kept = w_rows[n, pl.ds(core * half + i * step, step)].astype(F32)
            got = w_got[n, at].astype(F32)
            low, high = jnp.where(core == 0, kept, got), jnp.where(core == 0, got, kept)
            w_out[n, at] = jnp.concatenate([low, high], axis=1).astype(BF16)

    @pl.loop(0, N * N)
    def _(i):
        t, k = i // N, lax.rem(i, N)
        for n in range(6):
            arrived(par.at[n, t, k], par_send.at[n, t, k])

    @pl.loop(0, (N - 1) * N)
    def _(i):
        t, k = i // N, lax.rem(i, N)
        for n in range(6):
            arrived(r1.at[n, t, k], send1.at[n, t, k])
            arrived(r2.at[n, t, k], send2.at[n, t, k])

    for n in range(6):
        for j in range(N - 1):
            arrived(r3.at[n, j], send3.at[n, j])
    for n in range(4):
        arrived(g_send.at[n], swap_send.at[n])
        arrived(w_got.at[n], back_send.at[n])
    arrived(norm.at[0], norm_send.at[0, 0])
    for axis in range(3):
        for d in range(1, N):
            arrived(norm.at[0], norm_send.at[1 + axis, d - 1])


def scatter(g, w, m, v, tiles):
    half = tiles // 2
    any_, vmem = pl.BlockSpec(memory_space=pltpu.HBM), pl.BlockSpec(memory_space=pltpu.VMEM)
    dma = pltpu.SemaphoreType.DMA
    chunk = (N, half, 8, 128)
    return pl.pallas_call(
        scatter_kernel,
        out_shape=[
            jax.ShapeDtypeStruct((6, half, 8, 128), BF16),
            jax.ShapeDtypeStruct((4, tiles, 4, 128), BF16),
            jax.ShapeDtypeStruct((2, half, 8, 128), BF16),
            jax.ShapeDtypeStruct((8, 128), F32),
        ],
        in_specs=[any_] * 6 + [vmem] * 4,
        out_specs=[vmem] * 4,
        scratch_shapes=[
            pltpu.VMEM((N, 6, *chunk), BF16),
            pltpu.VMEM((6, N, N, *chunk), BF16),
            pltpu.VMEM((6, N - 1, N, *chunk), BF16),
            pltpu.VMEM((6, N - 1, *chunk), BF16),
            pltpu.VMEM((6, N - 1, half, 8, 128), BF16),
            pltpu.VMEM((4, half, 4, 128), BF16),
            pltpu.VMEM((4, tiles, 8, 128), BF16),
            pltpu.VMEM((2, half, 8, 128), BF16),
            pltpu.VMEM((4, tiles, 4, 128), BF16),
            pltpu.VMEM((4, half, 4, 128), BF16),
            pltpu.VMEM((5, 8, 128), F32),
            pltpu.VMEM((4, N - 1, 8, 128), F32),
            pltpu.VMEM((8, 128), F32),
            dma((N, 6)),
            dma((6, N, N)),
            dma((6, N, N)),
            dma((6, N - 1, N)),
            dma((6, N - 1, N)),
            dma((6, N - 1, N)),
            dma((6, N - 1, N)),
            dma((6, N - 1)),
            dma((6, N - 1)),
            dma((4, N - 1)),
            dma((4, N - 1)),
            dma((4,)),
            dma((4,)),
            dma((4,)),
            dma((4,)),
            dma((6,)),
        ],
        compiler_params=pltpu.CompilerParams(collective_id=0, has_side_effects=True, vmem_limit_bytes=67043328),
        name="scatter",
    )(*g, *w, m[0], m[1], v[0], v[1])


def gather_kernel(own, w0, w1, w2, local_sem, send_c, recv_c, send_b, recv_b, send_a, recv_a, send_p, recv_p):
    w = (w0, w1, w2)
    core, chip = place()
    half = own.shape[1]
    mine, theirs = pl.ds(core * half, half), pl.ds((1 - core) * half, half)
    partner = device(1 - core, chip)
    meet([partner] + [device(core, moved(chip, axis, by)) for axis in range(3) for by in (1, N - 1)])

    def at(n, i, j, k, tiles=mine):
        _, s, (a, b, c) = along(COLORS[n], chip)
        return block(w[COLORS[n][0]], COLORS[n], (back(a, s, i), back(b, s, j), None if k is None else back(c, s, k)), tiles)

    def to(n, phase):
        axes, s, _ = along(COLORS[n], chip)
        return device(core, moved(chip, axes[phase], s))

    for n in range(6):
        pltpu.make_async_copy(own.at[n], at(n, 0, 0, 0), local_sem.at[n]).start()
        send(own.at[n], at(n, 0, 0, 0), send_c.at[n, 0], recv_c.at[n, 0], to(n, 2))
        send(own.at[n], at(n, 0, 0, 0), send_b.at[n, 0, 0], recv_b.at[n, 0, 0], to(n, 1))
        send(own.at[n], at(n, 0, 0, 0), send_a.at[n, 0, 0, 0], recv_a.at[n, 0, 0, 0], to(n, 0))
        send(own.at[n], at(n, 0, 0, 0), send_p.at[n, 0, 0, 0], recv_p.at[n, 0, 0, 0], partner)

    def pass_on(n, i, j, k):
        here = at(n, i, j, k)
        send(here, here, send_a.at[n, i, j, k], recv_a.at[n, i, j, k], to(n, 0))
        send(here, here, send_p.at[n, i, j, k], recv_p.at[n, i, j, k], partner)

    def row(k):
        for n in range(6):
            here = at(n, 0, 0, k)
            arrived(here, recv_c.at[n, k - 1])

            @pl.when(k < N - 1)
            def _(n=n, here=here):
                send(here, here, send_c.at[n, k], recv_c.at[n, k], to(n, 2))

            send(here, here, send_b.at[n, 0, k], recv_b.at[n, 0, k], to(n, 1))
            pass_on(n, 0, 0, k)

    def plane(j, k):
        for n in range(6):
            here = at(n, 0, j, k)
            arrived(here, recv_b.at[n, j - 1, k])

            @pl.when(j < N - 1)
            def _(n=n, here=here):
                send(here, here, send_b.at[n, j, k], recv_b.at[n, j, k], to(n, 1))

            pass_on(n, 0, j, k)

    @pl.loop(1, 2 * N - 1)
    def _(far):
        @pl.loop(0, N)
        def _(j):
            k = far - j

            @pl.when((j == 0) & (k < N))
            def _():
                row(k)

            @pl.when((j > 0) & (k >= 0) & (k < N))
            def _():
                plane(j, k)

    def beyond(i, last):
        @pl.loop(0, N * N)
        def _(x):
            j, k = x // N, lax.rem(x, N)
            for n in range(6):
                here = at(n, i, j, k)
                arrived(here, recv_a.at[n, i - 1, j, k])
                if not last:
                    send(here, here, send_a.at[n, i, j, k], recv_a.at[n, i, j, k], to(n, 0))
                send(here, here, send_p.at[n, i, j, k], recv_p.at[n, i, j, k], partner)

    @pl.loop(1, N - 1)
    def _(i):
        beyond(i, False)

    beyond(N - 1, True)

    for n in range(6):
        here = at(n, 0, 0, 0)
        pltpu.make_async_copy(own.at[n], here, local_sem.at[n]).wait()
        for k in range(N - 1):
            arrived(here, send_c.at[n, k])

    @pl.loop(0, N * N)
    def _(x):
        j, k = x // N, lax.rem(x, N)
        for n in range(6):
            here = at(n, 0, j, k)

            @pl.when(j < N - 1)
            def _(n=n, here=here):
                arrived(here, send_b.at[n, j, k])

            for i in range(N):
                if i < N - 1:
                    arrived(here, send_a.at[n, i, j, k])
                arrived(here, send_p.at[n, i, j, k])
                arrived(at(n, i, j, k, theirs), recv_p.at[n, i, j, k])


def gather(own, tiles):
    any_, vmem = pl.BlockSpec(memory_space=pltpu.HBM), pl.BlockSpec(memory_space=pltpu.VMEM)
    dma = pltpu.SemaphoreType.DMA
    return pl.pallas_call(
        gather_kernel,
        out_shape=[jax.ShapeDtypeStruct((2, N, N, N, tiles, 8, 128), BF16)] * 3,
        in_specs=[vmem],
        out_specs=[any_] * 3,
        scratch_shapes=[
            dma((6,)),
            dma((6, N - 1)),
            dma((6, N - 1)),
            dma((6, N - 1, N)),
            dma((6, N - 1, N)),
            dma((6, N - 1, N, N)),
            dma((6, N - 1, N, N)),
            dma((6, N, N, N)),
            dma((6, N, N, N)),
        ],
        compiler_params=pltpu.CompilerParams(collective_id=1, has_side_effects=True),
        name="gather",
    )(own)


def wide_tiles(t, *major):
    rows = t.shape[-2] // functools.reduce(lambda a, b: a * b, major, 1)
    lead = t.shape[:-2]
    t = t.reshape(*lead, *major, rows, t.shape[-1] // 128, 128)
    return jnp.swapaxes(t, -3, -2)


def tall_tiles(t, *major):
    rows = t.shape[-2] // functools.reduce(lambda a, b: a * b, major, 1)
    lead = t.shape[:-2]
    t = t.reshape(*lead, *major, rows // 8, 8, t.shape[-1] // 128, 128)
    t = jnp.swapaxes(t, -3, -2)
    return t.reshape(*lead, *major, -1, 8, 128)


def from_wide(t, shape):
    return jnp.swapaxes(t, -3, -2).reshape(shape)


def from_tall(t, shape):
    columns = shape[-1] // 128
    t = t.reshape(*t.shape[:-3], t.shape[-3] // columns, columns, 8, 128)
    return jnp.swapaxes(t, -3, -2).reshape(shape)


def solution(mesh):
    def step(*arrays):
        terms, weights, m, v = (arrays[i : i + 3] for i in (0, 3, 6, 9))
        g = [wide_tiles(terms[0][0], N, N, N), wide_tiles(terms[1][0], N, N, N), tall_tiles(terms[2][0], N, N, N)]
        w = [wide_tiles(weights[0], N, N, N), wide_tiles(weights[1], N, N, N), tall_tiles(weights[2], N, N, N)]
        tiles = g[0].shape[4]

        def moments(one):
            return jnp.concatenate([wide_tiles(one[0]), wide_tiles(one[1])]), tall_tiles(one[2])

        own, g_wide, g_tall, factor = scatter(g, w, moments(m), moments(v), tiles)
        whole = gather(own, tiles)
        whole = [from_wide(whole[0], weights[0].shape), from_wide(whole[1], weights[1].shape), from_tall(whole[2], weights[2].shape)]
        grads = [from_wide(g_wide[:2], m[0].shape), from_wide(g_wide[2:], m[1].shape), from_tall(g_tall, m[2].shape)]
        grads = [one.astype(F32) * factor[0, 0] for one in grads]
        new_m = [0.9 * one + 0.1 * grad for one, grad in zip(m, grads, strict=True)]
        new_v = [0.95 * one + 0.05 * grad * grad for one, grad in zip(v, grads, strict=True)]
        return (*whole, *new_m, *new_v)

    all_of, cut = P(None, None, None), P(None, "dp", None)
    return jax.shard_map(
        step,
        mesh=mesh,
        in_specs=(P(("rep", "dp"), None, None, None),) * 3 + (all_of,) * 3 + (cut,) * 6,
        out_specs=(P("rep", None, None),) * 3 + (P("rep", "dp", None),) * 6,
        check_vma=False,
    )
```

time: 1310 us -> 282 us (0.22)
  waiting for transfers between devices: 1160 us -> 0 us
  Pallas kernels: 0 us -> 237 us
  blocking collectives: 69.3 us -> 0 us
  local copies, waits for them, and re-layouts: 52.5 us -> 35.2 us
  between operations: 16.5 us -> 0.67 us
    reduce_scatter x1 -> x0, waiting for transfers between devices: 663 us -> none  [step(): lax.psum_scatter(t[0], 'dp', scatter_dimension=1, tiled=True)]
    unnamed x6 -> x0, waiting for transfers between devices: 295 us -> none
    pallas_call x0 -> x2, Pallas kernels: none -> 237 us  [the longest x1 128 us: scatter(): pl.pallas_call(scatter_kernel, out_shape=[jax.ShapeDtypeStruct((6, half,...]
    all_gather x3 -> x0, waiting for transfers between devices: 200 us -> none  [step(): whole = [lax.all_gather(one[0], 'dp', axis=1, tiled=True) for one in new]]
    psum x1 -> x0, blocking collectives: 69.3 us -> none  [step(): squares = lax.psum(sum((jnp.sum(g * g) for g in gradients)), 'dp')]
    unnamed x15 -> x13, local copies, waits for them, and re-layouts: 50.9 us -> 34.1 us
  transfers between devices with their start and end apart: 5 -> 0, of which waited for: 5 -> 0; matrix products, arithmetic and copies ran while one was open for 3% -> 0% of each run, Pallas kernels for 0% -> 0%
where the time goes in v1:
time: 282 us
  Pallas kernels  237 us (84%)
  local copies, waits for them, and re-layouts  35.2 us (12%)
  other arithmetic  9.13 us (3%)
    pallas_call x1, Pallas kernels, scatter(): pl.pallas_call(scatter_kernel, out_shape=[jax.ShapeDtypeStruct((6, half,...  128 us
    pallas_call x1, Pallas kernels, gather(): pl.pallas_call(gather_kernel, out_shape=[jax.ShapeDtypeStruct((2, N, N, N...  109 us
    unnamed x13, local copies, waits for them, and re-layouts  34.1 us

profile of v1, /device:TPU:1, one launch (start us, length us, event | category | flops | bytes accessed | tf_op | source)
XLA Modules:
  0.0 281.8 jit_solution(10637132370566705033)
XLA Ops:
  0.6 2.4 pad_maximum_fusion
  3.0 127.6 %scatter.1 = (bf16[6,32,8,128]{3,2,1,0:T(8,128)(2,1)}, bf16[4,64,4,128]{3,2,1,0:T(4,128)(2,1)}, bf16[2,32,8,128]{3,2,1,0:T(8,128)(2,1)}, f32[8,128]{1,0:T(8,128)}) custom-call(bf16[2,4,4,4,64,8,128]{6,5,4,3,2,1,0:T(8,128)(2,1)} %bitcast.75, bf16[2,4,4,4,64,8,128]{6,5,4,3,2,1,0:T(8,128)(2,1)} %bitcast.76, bf16[2,4,4,4,64,8,128]{6,5,4,3,2,1,0:T(8,128)(2,1)} %bitcast.77, ...), custom_call_target="tpu_custom_call" | custom-call | tf_op jit(solution)/shard_map/scatter/pallas_call | solution.py:322
  130.6 109.1 %gather.1 = (bf16[2,4,4,4,64,8,128]{6,5,4,3,2,1,0:T(8,128)(2,1)}, bf16[2,4,4,4,64,8,128]{6,5,4,3,2,1,0:T(8,128)(2,1)}, bf16[2,4,4,4,64,8,128]{6,5,4,3,2,1,0:T(8,128)(2,1)}) custom-call(bf16[6,32,8,128]{3,2,1,0:T(8,128)(2,1)} %get-tuple-element.16.own), custom_call_target="tpu_custom_call" | custom-call | tf_op jit(solution)/shard_map/gather/pallas_call | solution.py:476
  239.8 1.2 slice.12
  240.9 3.2 %fusion.1 = (f32[2,4,8192]{2,1,0:T(4,128)}, f32[2,4,8192]{2,1,0:T(4,128)}, f32[2,4,8192]{2,1,0:T(4,128)}, f32[2,4,8192]{2,1,0:T(4,128)}) fusion(f32[2,4,8192]{2,1,0:T(4,128)} %param.22, f32[]{:T(128)} %bitcast.35, bf16[4,64,4,128]{3,2,1,0:T(4,128)(2,1)} %get-tuple-element.20, f32[2,4,8192]{2,1,0:T(4,128)} %param.19, f32[2,4,8192]{2,1,0:T(4,128)} %param.21, ...), kind=kLoop, calls=%fused_computation.6 | loop fusion | flops 1179648 | bytes 2359300 | tf_op jit(solution)/shard_map/add | solution.py:538
  244.2 1.6 convert_multiply_fusion
  245.8 1.9 fusion.2
  247.7 0.0 copy-start
  247.7 0.0 slice-start
  247.7 0.0 slice-start.1
  247.7 16.7 %copy.24 = bf16[2,512,8192]{2,1,0:T(8,128)(2,1)} copy(bf16[2,512,8192]{2,1,0:T(8,128)(2,1)} %bitcast.85) | data formatting | bytes 33554432
  264.4 0.0 copy-done
  264.4 0.0 slice-start.2
  264.4 0.0 slice-start.3
  264.4 8.5 %copy.25 = bf16[2,512,8192]{2,1,0:T(8,128)(2,1)} copy(bf16[2,512,8192]{2,1,0:T(8,128)(2,1)S(1)} %bitcast.84) | data formatting | bytes 33554432
  272.9 0.0 slice-done
  272.9 0.0 slice-done.1
  272.9 1.5 slice-done.2
  274.4 1.2 slice-done.3
  275.6 6.2 %copy.26 = bf16[2,8192,512]{2,1,0:T(8,128)(2,1)} copy(bf16[2,8192,512]{2,1,0:T(8,128)(2,1)S(1)} %bitcast.83) | data formatting | bytes 33554432
  (1 shorter events, 0.0 us)
Async XLA Ops:
  247.7 16.7 %copy-start = (bf16[2,4,4,4,64,8,128]{6,5,4,3,2,1,0:T(8,128)(2,1)S(1)}, bf16[2,4,4,4,64,8,128]{6,5,4,3,2,1,0:T(8,128)(2,1)}, u32[]{:S(2)}) copy-start(bf16[2,4,4,4,64,8,128]{6,5,4,3,2,1,0:T(8,128)(2,1)} %get-tuple-element.18) | copy-start | bytes 50331652
  247.7 25.2 %slice-start = ((s8[16777216]{0:T(1024)(128)(4,1)}), s8[4194304]{0:T(1024)(128)(4,1)S(1)}, s32[]{:S(2)}) async-start(s8[16777216]{0:T(1024)(128)(4,1)} %bitcast.81), calls=%async_computation | async-start | bytes 8388608
  247.7 25.2 %slice-start.1 = ((s8[16777216]{0:T(1024)(128)(4,1)}), s8[4194304]{0:T(1024)(128)(4,1)S(1)}, s32[]{:S(2)}) async-start(s8[16777216]{0:T(1024)(128)(4,1)} %bitcast.81), calls=%async_computation.1 | async-start | bytes 8388608
  264.4 10.0 %slice-start.2 = ((s8[16777216]{0:T(1024)(128)(4,1)}), s8[4194304]{0:T(1024)(128)(4,1)S(1)}, s32[]{:S(2)}) async-start(s8[16777216]{0:T(1024)(128)(4,1)} %bitcast.81), calls=%async_computation.2 | async-start | bytes 8388608
  264.4 11.2 %slice-start.3 = ((s8[16777216]{0:T(1024)(128)(4,1)}), s8[4194304]{0:T(1024)(128)(4,1)S(1)}, s32[]{:S(2)}) async-start(s8[16777216]{0:T(1024)(128)(4,1)} %bitcast.81), calls=%async_computation.3 | async-start | bytes 8388608

commit v2 on v1

v2 whole, which is shorter than its diff:
```python
import functools

import jax
import jax.numpy as jnp
from jax import lax
from jax.experimental import pallas as pl
from jax.experimental.pallas import tpu as pltpu
from jax.sharding import PartitionSpec as P

N = 4
AHEAD = 3
STEP = 8
STEP_LIMIT, FINISH_LIMIT = 10 * 2**20, 4 * 2**20
DEVICES = 2 * N**3
ORDERS = ((0, 1, 2), (1, 2, 0), (2, 0, 1))
COLORS = tuple((which, layer) for which in range(3) for layer in range(2))
F32, BF16 = jnp.float32, jnp.bfloat16


def place():
    me = lax.axis_index("dp")
    chip = me // 2
    return lax.rem(me, 2), (chip // (N * N), lax.rem(chip // N, N), lax.rem(chip, N))


def device(core, chip):
    return {"dp": ((chip[0] * N + chip[1]) * N + chip[2]) * 2 + core}


def moved(chip, axis, by):
    return tuple(lax.rem(c + by + N, N) if a == axis else c for a, c in enumerate(chip))


def along(color, chip):
    which, layer = color
    axes = ORDERS[which]
    return axes, 1 - 2 * layer, tuple(chip[a] for a in axes)


def back(c, s, by):
    return lax.rem(c - s * by + N, N)


def block(ref, color, abc, tiles):
    axes = ORDERS[color[0]]
    where = [slice(None)] * 3
    for a, c in zip(axes, abc, strict=True):
        if c is not None:
            where[a] = c
    return ref.at[(color[1], *where, tiles)]


def send(src, dst, send_sem, recv_sem, to):
    copy = pltpu.make_async_remote_copy(
        src_ref=src, dst_ref=dst, send_sem=send_sem, recv_sem=recv_sem, device_id=to, device_id_type=pl.DeviceIdType.MESH
    )
    copy.start()
    return copy


def arrived(ref, sem):
    pltpu.make_async_copy(ref, ref, sem).wait()


def meet(peers):
    barrier = pltpu.get_barrier_semaphore()
    for peer in peers:
        pl.semaphore_signal(barrier, inc=1, device_id=peer, device_id_type=pl.DeviceIdType.MESH)
    pl.semaphore_wait(barrier, len(peers))


def add_up(out, ins, step):
    @pl.loop(0, out.shape[0] // step)
    def _(n):
        at = pl.ds(n * step, step)
        total = ins[0][at].astype(F32)
        for one in ins[1:]:
            total = total + one[at].astype(F32)
        out[at] = total.astype(out.dtype)


def step_kernel(
    g0, g1, g2, w0, w1, w2, m0, m1, m2, v0, v1, v2,
    g_wide, g_tall, factor_out, whole,
    own, g_send, w_chip, w_chip_tall, w_rows, w_got, m_wide, m_tall, v_wide, v_tall, norm, norm_got,
    own_sem, par_send, par_recv, send1, recv1, send2, recv2, send3, recv3,
    norm_send, norm_recv, swap_send, swap_recv, back_send, back_recv, load_sem,
    send_c, recv_c, send_b, recv_b, send_a, recv_a, send_p, recv_p,
):
    g, w = (g0, g1, g2), (w0, w1, w2)
    core, chip = place()
    half = own.shape[3]
    step = min(STEP, half)
    mine, theirs = pl.ds(core * half, half), pl.ds((1 - core) * half, half)
    low, high = pl.ds(0, half), pl.ds(half, half)
    partner = device(1 - core, chip)

    def colored(n):
        return whole.at[COLORS[n][0], COLORS[n][1]]

    def par(n, t, k):
        return colored(n).at[t, k, :, low]

    def r1(n, t, k):
        return colored(n).at[t, k, :, high]

    def r2(n, k):
        return colored(n).at[N - 1, k, :, high]

    def r3(n, j):
        return colored(n).at[N - 1, N - 1, j, high]

    def blocks(n, count):
        if count < N:
            return colored(n).at[0, 0, pl.ds(0, count), low]
        if count < N * N:
            return colored(n).at[0, pl.ds(0, count // N), :, low]
        return colored(n).at[pl.ds(0, count // (N * N)), :, :, low]

    def to(n, phase):
        axes, s, _ = along(COLORS[n], chip)
        return device(core, moved(chip, axes[phase], s))

    def targets(color, t, k):
        axes, s, (a, b, c) = along(color, chip)
        return back(a, s, t + 1), back(b, s, k + 1), None

    def own_copy(n, t, k):
        return pltpu.make_async_copy(block(g[COLORS[n][0]], COLORS[n], targets(COLORS[n], t, k), mine), own.at[k, n], own_sem.at[k, n])

    def push(n, t, k):
        src = block(g[COLORS[n][0]], COLORS[n], targets(COLORS[n], t, k), theirs)
        send(src, par(n, t, k), par_send.at[n], par_recv.at[n, t, k], partner)

    @pl.loop(0, N)
    def _(k):
        for n in range(6):
            own_copy(n, 0, k).start()

    meet([partner] + [device(core, moved(chip, axis, by)) for axis in range(3) for by in range(1, N)])

    @pl.loop(0, AHEAD)
    def _(k):
        for n in range(6):
            push(n, 0, k)

    loads = []
    for n, (which, layer) in enumerate(COLORS):
        if which < 2:
            loads.append((block(w[which], COLORS[n], along(COLORS[n], chip)[2], slice(None)), w_chip.at[n]))
        else:
            loads.append((block(w[which], COLORS[n], along(COLORS[n], chip)[2], mine), w_chip_tall.at[layer]))
    loads += [(m0, m_wide.at[pl.ds(0, 2)]), (m1, m_wide.at[pl.ds(2, 2)]), (m2, m_tall)]
    loads += [(v0, v_wide.at[pl.ds(0, 2)]), (v1, v_wide.at[pl.ds(2, 2)]), (v2, v_tall)]
    loads = [pltpu.make_async_copy(src, dst, load_sem.at[i]) for i, (src, dst) in enumerate(loads)]
    for load in loads:
        load.start()

    def ready(n, t, k):
        own_copy(n, t, k).wait()
        arrived(par(n, t, k), par_recv.at[n, t, k])

    def first_axis(n, t, k, first):
        ready(n, t, k)
        ins = [own.at[k, n], par(n, t, k)]
        if not first:
            arrived(r1(n, t - 1, k), recv1.at[n, t - 1, k])
            ins.append(r1(n, t - 1, k))

        @pl.loop(0, N)
        def _(q):
            add_up(par(n, t, k).at[q], [one.at[q] for one in ins], step)

        send(par(n, t, k), r1(n, t, k), send1.at[n], recv1.at[n, t, k], to(n, 0))
        own_copy(n, t + 1, k).start()
        later = t * N + k + AHEAD
        push(n, later // N, lax.rem(later, N))

    @pl.loop(0, N)
    def _(k):
        for n in range(6):
            first_axis(n, 0, k, True)

    @pl.loop(0, 2 * N)
    def _(i):
        for n in range(6):
            first_axis(n, 1 + i // N, lax.rem(i, N), False)

    def second_axis(n, k, j, first):
        _, s, (_, _, c) = along(COLORS[n], chip)
        at = back(c, s, j + 1)
        ins = [own.at[k, n, at], par(n, N - 1, k).at[at], r1(n, N - 2, k).at[at]]
        if not first:
            arrived(r2(n, k - 1).at[at], recv2.at[n, k - 1, j])
            ins.append(r2(n, k - 1).at[at])
        out = par(n, N - 1, k).at[at]
        add_up(out, ins, step)
        send(out, r2(n, k).at[at], send2.at[n], recv2.at[n, k, j], to(n, 1))

    def second_axis_all(k, first):
        for n in range(6):
            @pl.when(k + AHEAD < N)
            def _(n=n):
                push(n, N - 1, k + AHEAD)

        for n in range(6):
            ready(n, N - 1, k)
            arrived(r1(n, N - 2, k), recv1.at[n, N - 2, k])

        @pl.loop(0, N)
        def _(j):
            for n in range(6):
                second_axis(n, k, j, first)

    second_axis_all(0, True)

    @pl.loop(1, N - 1)
    def _(k):
        second_axis_all(k, False)

    def third_axis_parts(n, j, first):
        _, s, (_, _, c) = along(COLORS[n], chip)
        k = N - 1
        at = back(c, s, j + 1)
        arrived(r2(n, k - 1).at[at], recv2.at[n, k - 1, j])
        ins = [own.at[k, n, at], par(n, N - 1, k).at[at], r1(n, N - 2, k).at[at], r2(n, k - 1).at[at]]
        if not first:
            arrived(r3(n, j - 1), recv3.at[n, j - 1])
            ins.append(r3(n, j - 1))
        return par(n, N - 1, k).at[at], ins

    def third_axis(n, j, first):
        out, ins = third_axis_parts(n, j, first)
        add_up(out, ins, step)
        send(out, r3(n, j), send3.at[n], recv3.at[n, j], to(n, 2))

    for n in range(6):
        ready(n, N - 1, N - 1)
        arrived(r1(n, N - 2, N - 1), recv1.at[n, N - 2, N - 1])
        third_axis(n, 0, True)

    @pl.loop(1, N - 1)
    def _(j):
        for n in range(6):
            third_axis(n, j, False)

    norm[0] = jnp.zeros(norm.shape[1:], F32)
    for n, (which, layer) in enumerate(COLORS):
        _, ins = third_axis_parts(n, N - 1, False)

        @pl.loop(0, half // step, init_carry=jnp.zeros(norm.shape[1:], F32))
        def squares(i, so_far, ins=ins, which=which, layer=layer, n=n):
            at = pl.ds(i * step, step)
            total = ins[0][at].astype(F32)
            for one in ins[1:]:
                total = total + one[at].astype(F32)
            rounded = total.astype(BF16)
            total = rounded.astype(F32)
            if which < 2:
                top, bottom = total[:, :4], total[:, 4:]
                g_wide[n, pl.ds(core * half + i * step, step)] = jnp.where(core == 0, top, bottom).astype(BF16)
                g_send[n, at] = jnp.where(core == 0, bottom, top).astype(BF16)
            else:
                g_tall[layer, at] = rounded
            return so_far + jnp.sum(total * total, axis=0)

        norm[0] += squares
        if which < 2:
            send(g_send.at[n], g_wide.at[n, mine], swap_send.at[n], swap_recv.at[n], partner)

    for n in range(6):
        arrived(blocks(n, (N - 1) * N * N), send1.at[n])
        arrived(blocks(n, (N - 1) * N), send2.at[n])
        arrived(blocks(n, N - 1), send3.at[n])

    send(norm.at[0], norm_got.at[0, 0], norm_send.at[0, 0], norm_recv.at[0, 0], partner)
    arrived(norm_got.at[0, 0], norm_recv.at[0, 0])
    norm[1] = norm[0] + norm_got[0, 0]
    for axis in range(3):
        for d in range(1, N):
            send(
                norm.at[1 + axis], norm_got.at[1 + axis, d - 1], norm_send.at[1 + axis, d - 1], norm_recv.at[1 + axis, d - 1],
                device(core, moved(chip, axis, d)),
            )
        if axis == 0:
            for load in loads:
                load.wait()
            for n in range(4):
                arrived(g_wide.at[n, theirs], swap_recv.at[n])
        total = norm[1 + axis]
        for d in range(1, N):
            arrived(norm_got.at[1 + axis, d - 1], norm_recv.at[1 + axis, d - 1])
            total = total + norm_got[1 + axis, d - 1]
        norm[2 + axis] = total
    count = 6 * N**3 * 2 * half * 8 * 128
    everything = jnp.sum(norm[4], keepdims=True)
    factor = jnp.minimum(1.0, 0.5 * lax.rsqrt(everything / count + 1e-30))
    factor_out[...] = jnp.broadcast_to(factor, factor_out.shape)

    def new_weight(old, m, v, grad):
        m = 0.9 * m + 0.1 * grad
        v = 0.95 * v + 0.05 * grad * grad
        return (old - 0.02 * (m * lax.rsqrt(v + 1e-8) + 0.1 * old)).astype(BF16)

    def at(n, i, j, k, tiles=mine):
        _, s, (a, b, c) = along(COLORS[n], chip)
        return block(whole.at[COLORS[n][0]], COLORS[n], (back(a, s, i), back(b, s, j), None if k is None else back(c, s, k)), tiles)

    def along_a(n, here, i, j):
        send(here, here, send_a.at[n], recv_a.at[n, i, j], to(n, 0))

    def along_b(n, here, j, k):
        send(here, here, send_b.at[n], recv_b.at[n, j, k], to(n, 1))

    def along_c(n, here, k):
        send(here, here, send_c.at[n], recv_c.at[n, k], to(n, 2))

    def across(n, here):
        send(here, here, send_p.at[n], recv_p.at[n], partner)

    def start(n):
        here = at(n, 0, 0, 0)
        along_c(n, here, 0)
        along_b(n, here, 0, 0)
        along_a(n, here, 0, 0)

    for n in range(4):

        @pl.loop(0, 2 * half // step)
        def _(i, n=n):
            at = pl.ds(i * step, step)
            old = w_chip[n, at].astype(F32)
            old = jnp.where(core == 0, old[:, :4], old[:, 4:])
            scale = jnp.broadcast_to(factor[:, :, None], old.shape)
            w_rows[n, at] = new_weight(old, m_wide[n, at], v_wide[n, at], g_wide[n, at].astype(F32) * scale)

        send(w_rows.at[n, theirs], w_got.at[n], back_send.at[n], back_recv.at[n], partner)

    for n in (4, 5):
        here = at(n, 0, 0, 0)

        @pl.loop(0, half // step)
        def _(i, layer=n - 4, here=here):
            at = pl.ds(i * step, step)
            old = w_chip_tall[layer, at].astype(F32)
            scale = jnp.broadcast_to(factor[:, :, None], old.shape)
            here[at] = new_weight(old, m_tall[layer, at], v_tall[layer, at], g_tall[layer, at].astype(F32) * scale)

        start(n)

    for n in range(4):
        here = at(n, 0, 0, 0)
        arrived(w_got.at[n], back_recv.at[n])

        @pl.loop(0, half // step)
        def _(i, n=n, here=here):
            at = pl.ds(i * step, step)
            kept = w_rows[n, pl.ds(core * half + i * step, step)].astype(F32)
            got = w_got[n, at].astype(F32)
            top, bottom = jnp.where(core == 0, kept, got), jnp.where(core == 0, got, kept)
            here[at] = jnp.concatenate([top, bottom], axis=1).astype(BF16)

        start(n)

    for n in range(6):
        across(n, at(n, 0, 0, 0))

    def row(k):
        for n in range(6):
            here = at(n, 0, 0, k)
            arrived(here, recv_c.at[n, k - 1])

            @pl.when(k < N - 1)
            def _(n=n, here=here):
                along_c(n, here, k)

            along_b(n, here, 0, k)
            along_a(n, here, 0, 0)
            across(n, here)

    def plane(j, k):
        for n in range(6):
            here = at(n, 0, j, k)
            arrived(here, recv_b.at[n, j - 1, k])

            @pl.when(j < N - 1)
            def _(n=n, here=here):
                along_b(n, here, j, k)

            along_a(n, here, 0, j)
            across(n, here)

    @pl.loop(1, 2 * N - 1)
    def _(far):
        @pl.loop(0, N)
        def _(j):
            k = far - j

            @pl.when((j == 0) & (k < N))
            def _():
                row(k)

            @pl.when((j > 0) & (k >= 0) & (k < N))
            def _():
                plane(j, k)

    def beyond(i, last):
        @pl.loop(0, N)
        def _(j):
            for n in range(6):
                here = at(n, i, j, None)
                arrived(here, recv_a.at[n, i - 1, j])
                if not last:
                    along_a(n, here, i, j)
                across(n, here)

    @pl.loop(1, N - 1)
    def _(i):
        beyond(i, False)

    for n in range(6):
        arrived(blocks(n, N**3), par_send.at[n])
    for n in range(4):
        arrived(g_send.at[n], swap_send.at[n])
        arrived(w_got.at[n], back_send.at[n])
    arrived(norm.at[0], norm_send.at[0, 0])
    for axis in range(3):
        for d in range(1, N):
            arrived(norm.at[0], norm_send.at[1 + axis, d - 1])

    beyond(N - 1, True)

    for n in range(6):
        arrived(blocks(n, N - 1), send_c.at[n])
        arrived(blocks(n, (N - 1) * N), send_b.at[n])
        arrived(blocks(n, (N - 1) * N * N), send_a.at[n])
        arrived(blocks(n, N**3), send_p.at[n])
        arrived(colored(n).at[:, :, :, theirs], recv_p.at[n])


def device_step(g, w, m, v, tiles):
    half = tiles // 2
    hbm, vmem = pl.BlockSpec(memory_space=pltpu.HBM), pl.BlockSpec(memory_space=pltpu.VMEM)
    dma = pltpu.SemaphoreType.DMA
    return pl.pallas_call(
        step_kernel,
        out_shape=[
            pltpu.VMEM((4, tiles, 4, 128), BF16),
            pltpu.VMEM((2, half, 8, 128), BF16),
            pltpu.VMEM((8, 128), F32),
            pltpu.VMEM((3, 2, N, N, N, tiles, 8, 128), BF16),
        ],
        in_specs=[hbm] * 12,
        out_specs=[vmem] * 4,
        scratch_shapes=[
            pltpu.VMEM((N, 6, N, half, 8, 128), BF16),
            pltpu.VMEM((4, half, 4, 128), BF16),
            pltpu.VMEM((4, tiles, 8, 128), BF16),
            pltpu.VMEM((2, half, 8, 128), BF16),
            pltpu.VMEM((4, tiles, 4, 128), BF16),
            pltpu.VMEM((4, half, 4, 128), BF16),
            pltpu.VMEM((4, tiles, 4, 128), F32),
            pltpu.VMEM((2, half, 8, 128), F32),
            pltpu.VMEM((4, tiles, 4, 128), F32),
            pltpu.VMEM((2, half, 8, 128), F32),
            pltpu.VMEM((5, 8, 128), F32),
            pltpu.VMEM((4, N - 1, 8, 128), F32),
            dma((N, 6)),
            dma((6,)),
            dma((6, N, N)),
            dma((6,)),
            dma((6, N - 1, N)),
            dma((6,)),
            dma((6, N - 1, N)),
            dma((6,)),
            dma((6, N - 1)),
            dma((4, N - 1)),
            dma((4, N - 1)),
            dma((4,)),
            dma((4,)),
            dma((4,)),
            dma((4,)),
            dma((12,)),
            dma((6,)),
            dma((6, N - 1)),
            dma((6,)),
            dma((6, N - 1, N)),
            dma((6,)),
            dma((6, N - 1, N)),
            dma((6,)),
            dma((6,)),
        ],
        compiler_params=pltpu.CompilerParams(collective_id=0, has_side_effects=True, vmem_limit_bytes=STEP_LIMIT),
        name="device_step",
    )(*g, *w, *m, *v)


def finish_kernel(w, g_wide, g_tall, factor, m0, m1, m2, v0, v1, v2, o0, o1, o2, nm0, nm1, nm2, nv0, nv1, nv2, sem):
    copies = [
        pltpu.make_async_copy(w.at[which, layer, x], dst.at[layer, x], sem.at[which, layer, x])
        for which, dst in enumerate((o0, o1, o2))
        for layer in range(2)
        for x in range(N)
    ]
    for copy in copies:
        copy.start()
    for which, (m, v, nm, nv) in enumerate(((m0, v0, nm0, nv0), (m1, v1, nm1, nv1), (m2, v2, nm2, nv2))):
        g = g_tall if which == 2 else g_wide.at[pl.ds(2 * which, 2)]
        for layer in range(2):

            @pl.loop(0, m.shape[1] // 8)
            def _(i, g=g, m=m, v=v, nm=nm, nv=nv, layer=layer):
                at = pl.ds(i * 8, 8)
                grad = g[layer, at].astype(F32)
                grad = grad * jnp.broadcast_to(factor[0:1, 0:1][:, :, None], grad.shape)
                nm[layer, at] = 0.9 * m[layer, at] + 0.1 * grad
                nv[layer, at] = 0.95 * v[layer, at] + 0.05 * grad * grad
    for copy in copies:
        copy.wait()


def finish(whole, g_wide, g_tall, factor, m, v):
    hbm, vmem = (pl.BlockSpec(memory_space=space) for space in (pltpu.HBM, pltpu.VMEM))
    whole_one = jax.ShapeDtypeStruct(whole.shape[1:], whole.dtype)
    like = [jax.ShapeDtypeStruct(one.shape, one.dtype) for one in (*[whole_one] * 3, *m, *v)]
    return pl.pallas_call(
        finish_kernel,
        out_shape=like,
        in_specs=[vmem] * 10,
        out_specs=[hbm] * 3 + [vmem] * 6,
        scratch_shapes=[pltpu.SemaphoreType.DMA((3, 2, N))],
        compiler_params=pltpu.CompilerParams(vmem_limit_bytes=FINISH_LIMIT),
        cost_estimate=pl.CostEstimate(flops=10**8, bytes_accessed=100 * 2**20, transcendentals=0),
        name="finish",
    )(whole, g_wide, g_tall, factor, *m, *v)


def wide_tiles(t, *major):
    rows = t.shape[-2] // functools.reduce(lambda a, b: a * b, major, 1)
    lead = t.shape[:-2]
    t = t.reshape(*lead, *major, rows, t.shape[-1] // 128, 128)
    return jnp.swapaxes(t, -3, -2)


def tall_tiles(t, *major):
    rows = t.shape[-2] // functools.reduce(lambda a, b: a * b, major, 1)
    lead = t.shape[:-2]
    t = t.reshape(*lead, *major, rows // 8, 8, t.shape[-1] // 128, 128)
    t = jnp.swapaxes(t, -3, -2)
    return t.reshape(*lead, *major, -1, 8, 128)


def from_wide(t, shape):
    return jnp.swapaxes(t, -3, -2).reshape(shape)


def from_tall(t, shape):
    columns = shape[-1] // 128
    t = t.reshape(*t.shape[:-3], t.shape[-3] // columns, columns, 8, 128)
    return jnp.swapaxes(t, -3, -2).reshape(shape)


def solution(mesh):
    def step(*arrays):
        terms, weights, m, v = (arrays[i : i + 3] for i in (0, 3, 6, 9))
        g = [wide_tiles(terms[0][0], N, N, N), wide_tiles(terms[1][0], N, N, N), tall_tiles(terms[2][0], N, N, N)]
        w = [wide_tiles(weights[0], N, N, N), wide_tiles(weights[1], N, N, N), tall_tiles(weights[2], N, N, N)]
        tiles = g[0].shape[4]

        def moments(one):
            return wide_tiles(one[0]), wide_tiles(one[1]), tall_tiles(one[2])

        m, v = moments(m), moments(v)
        g_wide, g_tall, factor, whole = device_step(g, w, m, v, tiles)
        new = finish(whole, g_wide, g_tall, factor, m, v)
        shapes = [one.shape for one in arrays[3:]]
        return tuple((from_tall if i % 3 == 2 else from_wide)(one, shape) for i, (one, shape) in enumerate(zip(new, shapes, strict=True)))

    all_of, cut = P(None, None, None), P(None, "dp", None)
    return jax.shard_map(
        step,
        mesh=mesh,
        in_specs=(P(("rep", "dp"), None, None, None),) * 3 + (all_of,) * 3 + (cut,) * 6,
        out_specs=(P("rep", None, None),) * 3 + (P("rep", "dp", None),) * 6,
        check_vma=False,
    )
```

time: 282 us -> 236 us (0.84)
  local copies, waits for them, and re-layouts: 35.2 us -> 0.03 us
  other arithmetic: 9.13 us -> 0 us
    unnamed x13 -> x12, local copies, waits for them, and re-layouts: 34.1 us -> 0.03 us
    add x2 -> x0, other arithmetic: 5.16 us -> none  [step(): 0.95 * one + 0.05 * grad * grad]
where the time goes in v2:
time: 236 us
  Pallas kernels  236 us (100%)
    pallas_call x1, Pallas kernels, device_step(): pl.pallas_call(step_kernel, out_shape=[pltpu.VMEM((4, tiles, 4, 128), BF1...  218 us
    pallas_call x1, Pallas kernels, finish(): pl.pallas_call(finish_kernel, out_shape=like, in_specs=[vmem] * 10, out_s...  17.3 us

profile of v2, /device:TPU:1, one launch (start us, length us, event | category | flops | bytes accessed | tf_op | source)
XLA Modules:
  0.0 236.3 jit_solution(949088873698727805)
XLA Ops:
  0.6 0.0 copy-start
  0.7 0.0 copy-start.1
  0.7 0.0 copy-start.2
  0.7 0.0 copy-start.3
  0.7 0.0 copy-start.4
  0.7 0.0 copy-start.5
  0.7 218.3 %device_step.1 = (bf16[4,64,4,128]{3,2,1,0:T(4,128)(2,1)S(1)}, bf16[2,32,8,128]{3,2,1,0:T(8,128)(2,1)S(1)}, f32[8,128]{1,0:T(8,128)S(1)}, bf16[3,2,4,4,4,64,8,128]{7,6,5,4,3,2,1,0:T(8,128)(2,1)S(1)}) custom-call(bf16[2,4,4,4,64,8,128]{6,5,4,3,2,1,0:T(8,128)(2,1)} %bitcast.89, bf16[2,4,4,4,64,8,128]{6,5,4,3,2,1,0:T(8,128)(2,1)} %bitcast.90, ...), custom_call_target="tpu_custom_call" | custom-call | tf_op jit(solution)/shard_map/device_step/pallas_call | solution.py:445
  219.0 0.0 copy-done
  219.0 0.0 copy-done.1
  219.0 0.0 copy-done.2
  219.0 0.0 copy-done.3
  219.0 0.0 copy-done.4
  219.0 0.0 copy-done.5
  219.0 17.3 %finish.1 = (bf16[2,4,4,4,64,8,128]{6,5,4,3,2,1,0:T(8,128)(2,1)}, bf16[2,4,4,4,64,8,128]{6,5,4,3,2,1,0:T(8,128)(2,1)}, bf16[2,4,4,4,64,8,128]{6,5,4,3,2,1,0:T(8,...) custom-call(bf16[3,2,4,4,4,64,8,128]{7,6,5,4,3,2,1,0:T(8,128)(2,1)S(, ...), custom_call_target="tpu_custom_call" | custom-call | flops 100000000 | bytes 104857600 | tf_op jit(solution)/shard_map/finish/pallas_call | solution.py:526
Async XLA Ops:
  0.6 218.3 %copy-start = (f32[2,4,8192]{2,1,0:T(4,128)S(1)}, f32[2,4,8192]{2,1,0:T(4,128)}, u32[]{:S(2)}) copy-start(f32[2,4,8192]{2,1,0:T(4,128)} %param.18) | copy-start | bytes 786436
  0.7 218.3 %copy-start.1 = (f32[2,4,8192]{2,1,0:T(4,128)S(1)}, f32[2,4,8192]{2,1,0:T(4,128)}, u32[]{:S(2)}) copy-start(f32[2,4,8192]{2,1,0:T(4,128)} %param.19) | copy-start | bytes 786436
  0.7 218.3 %copy-start.2 = (f32[2,64,512]{2,1,0:T(8,128)S(1)}, f32[2,64,512]{2,1,0:T(8,128)}, u32[]{:S(2)}) copy-start(f32[2,64,512]{2,1,0:T(8,128)} %param.20) | copy-start | bytes 786436
  0.7 218.3 %copy-start.3 = (f32[2,4,8192]{2,1,0:T(4,128)S(1)}, f32[2,4,8192]{2,1,0:T(4,128)}, u32[]{:S(2)}) copy-start(f32[2,4,8192]{2,1,0:T(4,128)} %param.21) | copy-start | bytes 786436
  0.7 218.3 %copy-start.4 = (f32[2,4,8192]{2,1,0:T(4,128)S(1)}, f32[2,4,8192]{2,1,0:T(4,128)}, u32[]{:S(2)}) copy-start(f32[2,4,8192]{2,1,0:T(4,128)} %param.22) | copy-start | bytes 786436
  0.7 218.3 %copy-start.5 = (f32[2,64,512]{2,1,0:T(8,128)S(1)}, f32[2,64,512]{2,1,0:T(8,128)}, u32[]{:S(2)}) copy-start(f32[2,64,512]{2,1,0:T(8,128)} %param.23) | copy-start | bytes 786436

commit v3 on v2

--- a/solution.py
+++ b/solution.py
@@ -8,7 +8,7 @@
 from jax.sharding import PartitionSpec as P
 
 N = 4
-AHEAD = 3
+AHEAD = 2
 STEP = 8
 STEP_LIMIT, FINISH_LIMIT = 10 * 2**20, 4 * 2**20
 DEVICES = 2 * N**3
@@ -81,11 +81,10 @@
 
 def step_kernel(
     g0, g1, g2, w0, w1, w2, m0, m1, m2, v0, v1, v2,
-    g_wide, g_tall, factor_out, whole,
-    own, g_send, w_chip, w_chip_tall, w_rows, w_got, m_wide, m_tall, v_wide, v_tall, norm, norm_got,
+    m_wide, m_tall, v_wide, v_tall, whole,
+    own, g_send, g_wide, g_tall, w_chip, w_chip_tall, w_rows, w_got, norm, norm_got,
     own_sem, par_send, par_recv, send1, recv1, send2, recv2, send3, recv3,
-    norm_send, norm_recv, swap_send, swap_recv, back_send, back_recv, load_sem,
-    send_c, recv_c, send_b, recv_b, send_a, recv_a, send_p, recv_p,
+    norm_send, norm_recv, swap_send, swap_recv, back_send, back_recv, load_sem, send_p, recv_p,
 ):
     g, w = (g0, g1, g2), (w0, w1, w2)
     core, chip = place()
@@ -126,13 +125,13 @@
         return back(a, s, t + 1), back(b, s, k + 1), None
 
     def own_copy(n, t, k):
-        return pltpu.make_async_copy(block(g[COLORS[n][0]], COLORS[n], targets(COLORS[n], t, k), mine), own.at[k, n], own_sem.at[k, n])
+        return pltpu.make_async_copy(block(g[COLORS[n][0]], COLORS[n], targets(COLORS[n], t, k), mine), own.at[k, n], own_sem.at[lax.rem(k, AHEAD), n])
 
     def push(n, t, k):
         src = block(g[COLORS[n][0]], COLORS[n], targets(COLORS[n], t, k), theirs)
-        send(src, par(n, t, k), par_send.at[n], par_recv.at[n, t, k], partner)
-
-    @pl.loop(0, N)
+        send(src, par(n, t, k), par_send.at[n], par_recv.at[n, k], partner)
+
+    @pl.loop(0, AHEAD)
     def _(k):
         for n in range(6):
             own_copy(n, 0, k).start()
@@ -147,18 +146,21 @@
     loads = []
     for n, (which, layer) in enumerate(COLORS):
         if which < 2:
-            loads.append((block(w[which], COLORS[n], along(COLORS[n], chip)[2], slice(None)), w_chip.at[n]))
+            loads.append((block(w[which], COLORS[n], along(COLORS[n], chip)[2], slice(None)), w_chip.at[n], 0))
         else:
-            loads.append((block(w[which], COLORS[n], along(COLORS[n], chip)[2], mine), w_chip_tall.at[layer]))
-    loads += [(m0, m_wide.at[pl.ds(0, 2)]), (m1, m_wide.at[pl.ds(2, 2)]), (m2, m_tall)]
-    loads += [(v0, v_wide.at[pl.ds(0, 2)]), (v1, v_wide.at[pl.ds(2, 2)]), (v2, v_tall)]
-    loads = [pltpu.make_async_copy(src, dst, load_sem.at[i]) for i, (src, dst) in enumerate(loads)]
-    for load in loads:
-        load.start()
+            loads.append((block(w[which], COLORS[n], along(COLORS[n], chip)[2], mine), w_chip_tall.at[layer], 1))
+    loads += [(m0, m_wide.at[pl.ds(0, 2)], 2), (m1, m_wide.at[pl.ds(2, 2)], 2), (m2, m_tall, 3)]
+    loads += [(v0, v_wide.at[pl.ds(0, 2)], 4), (v1, v_wide.at[pl.ds(2, 2)], 4), (v2, v_tall, 5)]
+    for src, dst, i in loads:
+        pltpu.make_async_copy(src, dst, load_sem.at[i]).start()
+
+    def ask(n, i):
+        own_copy(n, i // N, lax.rem(i, N)).start()
+        push(n, i // N, lax.rem(i, N))
 
     def ready(n, t, k):
         own_copy(n, t, k).wait()
-        arrived(par(n, t, k), par_recv.at[n, t, k])
+        arrived(par(n, t, k), par_recv.at[n, k])
 
     def first_axis(n, t, k, first):
         ready(n, t, k)
@@ -172,9 +174,7 @@
             add_up(par(n, t, k).at[q], [one.at[q] for one in ins], step)
 
         send(par(n, t, k), r1(n, t, k), send1.at[n], recv1.at[n, t, k], to(n, 0))
-        own_copy(n, t + 1, k).start()
-        later = t * N + k + AHEAD
-        push(n, later // N, lax.rem(later, N))
+        ask(n, t * N + k + AHEAD)
 
     @pl.loop(0, N)
     def _(k):
@@ -186,9 +186,12 @@
         for n in range(6):
             first_axis(n, 1 + i // N, lax.rem(i, N), False)
 
+    def place_of(n, j):
+        _, s, (_, _, c) = along(COLORS[n], chip)
+        return back(c, s, j + 1 + (1 - j // 2) * (1 - 2 * j))
+
     def second_axis(n, k, j, first):
-        _, s, (_, _, c) = along(COLORS[n], chip)
-        at = back(c, s, j + 1)
+        at = place_of(n, j)
         ins = [own.at[k, n, at], par(n, N - 1, k).at[at], r1(n, N - 2, k).at[at]]
         if not first:
             arrived(r2(n, k - 1).at[at], recv2.at[n, k - 1, j])
@@ -199,13 +202,12 @@
 
     def second_axis_all(k, first):
         for n in range(6):
+            ready(n, N - 1, k)
+            arrived(r1(n, N - 2, k), recv1.at[n, N - 2, k])
+
             @pl.when(k + AHEAD < N)
             def _(n=n):
-                push(n, N - 1, k + AHEAD)
-
-        for n in range(6):
-            ready(n, N - 1, k)
-            arrived(r1(n, N - 2, k), recv1.at[n, N - 2, k])
+                ask(n, (N - 1) * N + k + AHEAD)
 
         @pl.loop(0, N)
         def _(j):
@@ -218,35 +220,50 @@
     def _(k):
         second_axis_all(k, False)
 
-    def third_axis_parts(n, j, first):
-        _, s, (_, _, c) = along(COLORS[n], chip)
+    def third_axis_parts(n, j):
         k = N - 1
-        at = back(c, s, j + 1)
+        at = place_of(n, j)
         arrived(r2(n, k - 1).at[at], recv2.at[n, k - 1, j])
-        ins = [own.at[k, n, at], par(n, N - 1, k).at[at], r1(n, N - 2, k).at[at], r2(n, k - 1).at[at]]
-        if not first:
-            arrived(r3(n, j - 1), recv3.at[n, j - 1])
-            ins.append(r3(n, j - 1))
-        return par(n, N - 1, k).at[at], ins
-
-    def third_axis(n, j, first):
-        out, ins = third_axis_parts(n, j, first)
-        add_up(out, ins, step)
-        send(out, r3(n, j), send3.at[n], recv3.at[n, j], to(n, 2))
-
-    for n in range(6):
+        return [par(n, N - 1, k).at[at], own.at[k, n, at], r1(n, N - 2, k).at[at], r2(n, k - 1).at[at]]
+
+    quarter = half // 2
+    first_half, second_half = pl.ds(0, quarter), pl.ds(quarter, quarter)
+
+    def to_third(n, s):
+        return device(core, moved(chip, along(COLORS[n], chip)[0][2], s))
+
+    def third_axis(n, parts, tiles, slot, sem, way, more=None):
+        out = parts[0].at[tiles]
+        add_up(out, [one.at[tiles] for one in parts] + ([] if more is None else [more]), step)
+        send(out, r3(n, slot).at[tiles], send3.at[n], recv3.at[n, sem], to_third(n, way))
+
+    up, down = [], []
+    for n in range(6):
+        s = 1 - 2 * COLORS[n][1]
         ready(n, N - 1, N - 1)
         arrived(r1(n, N - 2, N - 1), recv1.at[n, N - 2, N - 1])
-        third_axis(n, 0, True)
-
-    @pl.loop(1, N - 1)
-    def _(j):
-        for n in range(6):
-            third_axis(n, j, False)
+        parts = third_axis_parts(n, 0)
+        third_axis(n, parts, first_half, 0, 0, s)
+        third_axis(n, parts, second_half, 0, 1, -s)
+    for n in range(6):
+        s = 1 - 2 * COLORS[n][1]
+        up.append(third_axis_parts(n, 1))
+        third_axis(n, up[n], first_half, 2, 3, -s)
+        down.append(third_axis_parts(n, 2))
+        third_axis(n, down[n], second_half, 1, 2, s)
+    for n in range(6):
+        s = 1 - 2 * COLORS[n][1]
+        arrived(r3(n, 0).at[first_half], recv3.at[n, 0])
+        third_axis(n, down[n], first_half, 1, 2, s, r3(n, 0).at[first_half])
+        arrived(r3(n, 0).at[second_half], recv3.at[n, 1])
+        third_axis(n, up[n], second_half, 2, 3, -s, r3(n, 0).at[second_half])
 
     norm[0] = jnp.zeros(norm.shape[1:], F32)
     for n, (which, layer) in enumerate(COLORS):
-        _, ins = third_axis_parts(n, N - 1, False)
+        ins = third_axis_parts(n, 3)
+        for slot in (1, 2):
+            arrived(r3(n, slot), recv3.at[n, slot + 1])
+            ins.append(r3(n, slot))
 
         @pl.loop(0, half // step, init_carry=jnp.zeros(norm.shape[1:], F32))
         def squares(i, so_far, ins=ins, which=which, layer=layer, n=n):
@@ -266,54 +283,50 @@
 
         norm[0] += squares
         if which < 2:
-            send(g_send.at[n], g_wide.at[n, mine], swap_send.at[n], swap_recv.at[n], partner)
+            send(g_send.at[n], g_wide.at[n, mine], swap_send, swap_recv, partner)
 
     for n in range(6):
         arrived(blocks(n, (N - 1) * N * N), send1.at[n])
         arrived(blocks(n, (N - 1) * N), send2.at[n])
         arrived(blocks(n, N - 1), send3.at[n])
 
-    send(norm.at[0], norm_got.at[0, 0], norm_send.at[0, 0], norm_recv.at[0, 0], partner)
-    arrived(norm_got.at[0, 0], norm_recv.at[0, 0])
+    send(norm.at[0], norm_got.at[0, 0], norm_send.at[0], norm_recv.at[0], partner)
+    arrived(norm_got.at[0, 0], norm_recv.at[0])
     norm[1] = norm[0] + norm_got[0, 0]
     for axis in range(3):
         for d in range(1, N):
-            send(
-                norm.at[1 + axis], norm_got.at[1 + axis, d - 1], norm_send.at[1 + axis, d - 1], norm_recv.at[1 + axis, d - 1],
-                device(core, moved(chip, axis, d)),
-            )
+            src, dst = norm.at[1 + axis], norm_got.at[1 + axis, d - 1]
+            send(src, dst, norm_send.at[1], norm_recv.at[1 + axis], device(core, moved(chip, axis, d)))
         if axis == 0:
-            for load in loads:
-                load.wait()
-            for n in range(4):
-                arrived(g_wide.at[n, theirs], swap_recv.at[n])
+            for i, dst in enumerate((w_chip, w_chip_tall, m_wide, m_tall, v_wide, v_tall)):
+                arrived(dst, load_sem.at[i])
+            arrived(g_wide.at[:, theirs], swap_recv)
+        arrived(norm_got.at[1 + axis], norm_recv.at[1 + axis])
         total = norm[1 + axis]
         for d in range(1, N):
-            arrived(norm_got.at[1 + axis, d - 1], norm_recv.at[1 + axis, d - 1])
             total = total + norm_got[1 + axis, d - 1]
         norm[2 + axis] = total
     count = 6 * N**3 * 2 * half * 8 * 128
     everything = jnp.sum(norm[4], keepdims=True)
     factor = jnp.minimum(1.0, 0.5 * lax.rsqrt(everything / count + 1e-30))
-    factor_out[...] = jnp.broadcast_to(factor, factor_out.shape)
 
     def new_weight(old, m, v, grad):
         m = 0.9 * m + 0.1 * grad
         v = 0.95 * v + 0.05 * grad * grad
-        return (old - 0.02 * (m * lax.rsqrt(v + 1e-8) + 0.1 * old)).astype(BF16)
+        return (old - 0.02 * (m * lax.rsqrt(v + 1e-8) + 0.1 * old)).astype(BF16), m, v
 
     def at(n, i, j, k, tiles=mine):
         _, s, (a, b, c) = along(COLORS[n], chip)
         return block(whole.at[COLORS[n][0]], COLORS[n], (back(a, s, i), back(b, s, j), None if k is None else back(c, s, k)), tiles)
 
     def along_a(n, here, i, j):
-        send(here, here, send_a.at[n], recv_a.at[n, i, j], to(n, 0))
+        send(here, here, send1.at[n], recv1.at[n, i, j], to(n, 0))
 
     def along_b(n, here, j, k):
-        send(here, here, send_b.at[n], recv_b.at[n, j, k], to(n, 1))
+        send(here, here, send2.at[n], recv2.at[n, j, k], to(n, 1))
 
     def along_c(n, here, k):
-        send(here, here, send_c.at[n], recv_c.at[n, k], to(n, 2))
+        send(here, here, send3.at[n], recv3.at[n, k], to(n, 2))
 
     def across(n, here):
         send(here, here, send_p.at[n], recv_p.at[n], partner)
@@ -332,9 +345,9 @@
             old = w_chip[n, at].astype(F32)
             old = jnp.where(core == 0, old[:, :4], old[:, 4:])
             scale = jnp.broadcast_to(factor[:, :, None], old.shape)
-            w_rows[n, at] = new_weight(old, m_wide[n, at], v_wide[n, at], g_wide[n, at].astype(F32) * scale)
-
-        send(w_rows.at[n, theirs], w_got.at[n], back_send.at[n], back_recv.at[n], partner)
+            w_rows[n, at], m_wide[n, at], v_wide[n, at] = new_weight(old, m_wide[n, at], v_wide[n, at], g_wide[n, at].astype(F32) * scale)
+
+        send(w_rows.at[n, theirs], w_got.at[n], back_send, back_recv.at[n], partner)
 
     for n in (4, 5):
         here = at(n, 0, 0, 0)
@@ -344,7 +357,7 @@
             at = pl.ds(i * step, step)
             old = w_chip_tall[layer, at].astype(F32)
             scale = jnp.broadcast_to(factor[:, :, None], old.shape)
-            here[at] = new_weight(old, m_tall[layer, at], v_tall[layer, at], g_tall[layer, at].astype(F32) * scale)
+            here[at], m_tall[layer, at], v_tall[layer, at] = new_weight(old, m_tall[layer, at], v_tall[layer, at], g_tall[layer, at].astype(F32) * scale)
 
         start(n)
 
@@ -368,7 +381,7 @@
     def row(k):
         for n in range(6):
             here = at(n, 0, 0, k)
-            arrived(here, recv_c.at[n, k - 1])
+            arrived(here, recv3.at[n, k - 1])
 
             @pl.when(k < N - 1)
             def _(n=n, here=here):
@@ -381,7 +394,7 @@
     def plane(j, k):
         for n in range(6):
             here = at(n, 0, j, k)
-            arrived(here, recv_b.at[n, j - 1, k])
+            arrived(here, recv2.at[n, j - 1, k])
 
             @pl.when(j < N - 1)
             def _(n=n, here=here):
@@ -409,7 +422,7 @@
         def _(j):
             for n in range(6):
                 here = at(n, i, j, None)
-                arrived(here, recv_a.at[n, i - 1, j])
+                arrived(here, recv1.at[n, i - 1, j])
                 if not last:
                     along_a(n, here, i, j)
                 across(n, here)
@@ -420,20 +433,17 @@
 
     for n in range(6):
         arrived(blocks(n, N**3), par_send.at[n])
-    for n in range(4):
-        arrived(g_send.at[n], swap_send.at[n])
-        arrived(w_got.at[n], back_send.at[n])
-    arrived(norm.at[0], norm_send.at[0, 0])
-    for axis in range(3):
-        for d in range(1, N):
-            arrived(norm.at[0], norm_send.at[1 + axis, d - 1])
+    arrived(g_send, swap_send)
+    arrived(w_got, back_send)
+    arrived(norm.at[0], norm_send.at[0])
+    arrived(norm_got.at[pl.ds(1, 3)], norm_send.at[1])
 
     beyond(N - 1, True)
 
     for n in range(6):
-        arrived(blocks(n, N - 1), send_c.at[n])
-        arrived(blocks(n, (N - 1) * N), send_b.at[n])
-        arrived(blocks(n, (N - 1) * N * N), send_a.at[n])
+        arrived(blocks(n, N - 1), send3.at[n])
+        arrived(blocks(n, (N - 1) * N), send2.at[n])
+        arrived(blocks(n, (N - 1) * N * N), send1.at[n])
         arrived(blocks(n, N**3), send_p.at[n])
         arrived(colored(n).at[:, :, :, theirs], recv_p.at[n])
 
@@ -445,48 +455,41 @@
     return pl.pallas_call(
         step_kernel,
         out_shape=[
-            pltpu.VMEM((4, tiles, 4, 128), BF16),
-            pltpu.VMEM((2, half, 8, 128), BF16),
-            pltpu.VMEM((8, 128), F32),
+            pltpu.VMEM((4, tiles, 4, 128), F32),
+            pltpu.VMEM((2, half, 8, 128), F32),
+            pltpu.VMEM((4, tiles, 4, 128), F32),
+            pltpu.VMEM((2, half, 8, 128), F32),
             pltpu.VMEM((3, 2, N, N, N, tiles, 8, 128), BF16),
         ],
         in_specs=[hbm] * 12,
-        out_specs=[vmem] * 4,
+        out_specs=[vmem] * 5,
         scratch_shapes=[
             pltpu.VMEM((N, 6, N, half, 8, 128), BF16),
             pltpu.VMEM((4, half, 4, 128), BF16),
+            pltpu.VMEM((4, tiles, 4, 128), BF16),
+            pltpu.VMEM((2, half, 8, 128), BF16),
             pltpu.VMEM((4, tiles, 8, 128), BF16),
             pltpu.VMEM((2, half, 8, 128), BF16),
             pltpu.VMEM((4, tiles, 4, 128), BF16),
             pltpu.VMEM((4, half, 4, 128), BF16),
-            pltpu.VMEM((4, tiles, 4, 128), F32),
-            pltpu.VMEM((2, half, 8, 128), F32),
-            pltpu.VMEM((4, tiles, 4, 128), F32),
-            pltpu.VMEM((2, half, 8, 128), F32),
             pltpu.VMEM((5, 8, 128), F32),
             pltpu.VMEM((4, N - 1, 8, 128), F32),
-            dma((N, 6)),
-            dma((6,)),
-            dma((6, N, N)),
+            dma((AHEAD, 6)),
+            dma((6,)),
+            dma((6, N)),
             dma((6,)),
             dma((6, N - 1, N)),
             dma((6,)),
             dma((6, N - 1, N)),
             dma((6,)),
-            dma((6, N - 1)),
-            dma((4, N - 1)),
-            dma((4, N - 1)),
+            dma((6, 4)),
+            dma((2,)),
             dma((4,)),
+            dma,
+            dma,
+            dma,
             dma((4,)),
-            dma((4,)),
-            dma((4,)),
-            dma((12,)),
-            dma((6,)),
-            dma((6, N - 1)),
-            dma((6,)),
-            dma((6, N - 1, N)),
-            dma((6,)),
-            dma((6, N - 1, N)),
+            dma((6,)),
             dma((6,)),
             dma((6,)),
         ],
@@ -495,44 +498,31 @@
     )(*g, *w, *m, *v)
 
 
-def finish_kernel(w, g_wide, g_tall, factor, m0, m1, m2, v0, v1, v2, o0, o1, o2, nm0, nm1, nm2, nv0, nv1, nv2, sem):
-    copies = [
-        pltpu.make_async_copy(w.at[which, layer, x], dst.at[layer, x], sem.at[which, layer, x])
-        for which, dst in enumerate((o0, o1, o2))
-        for layer in range(2)
-        for x in range(N)
-    ]
+def finish_kernel(m_wide, m_tall, v_wide, v_tall, w, *refs):
+    out, sem = refs[:-1], refs[-1]
+    copies = [(w.at[which, layer, x], out[which].at[layer, x]) for which in range(3) for layer in range(2) for x in range(N)]
+    for first, wide, tall in ((3, m_wide, m_tall), (6, v_wide, v_tall)):
+        copies += [(wide.at[pl.ds(0, 2)], out[first]), (wide.at[pl.ds(2, 2)], out[first + 1]), (tall, out[first + 2])]
+    copies = [pltpu.make_async_copy(src, dst, sem.at[i]) for i, (src, dst) in enumerate(copies)]
     for copy in copies:
         copy.start()
-    for which, (m, v, nm, nv) in enumerate(((m0, v0, nm0, nv0), (m1, v1, nm1, nv1), (m2, v2, nm2, nv2))):
-        g = g_tall if which == 2 else g_wide.at[pl.ds(2 * which, 2)]
-        for layer in range(2):
-
-            @pl.loop(0, m.shape[1] // 8)
-            def _(i, g=g, m=m, v=v, nm=nm, nv=nv, layer=layer):
-                at = pl.ds(i * 8, 8)
-                grad = g[layer, at].astype(F32)
-                grad = grad * jnp.broadcast_to(factor[0:1, 0:1][:, :, None], grad.shape)
-                nm[layer, at] = 0.9 * m[layer, at] + 0.1 * grad
-                nv[layer, at] = 0.95 * v[layer, at] + 0.05 * grad * grad
     for copy in copies:
         copy.wait()
 
 
-def finish(whole, g_wide, g_tall, factor, m, v):
+def finish(moments, whole, like):
     hbm, vmem = (pl.BlockSpec(memory_space=space) for space in (pltpu.HBM, pltpu.VMEM))
-    whole_one = jax.ShapeDtypeStruct(whole.shape[1:], whole.dtype)
-    like = [jax.ShapeDtypeStruct(one.shape, one.dtype) for one in (*[whole_one] * 3, *m, *v)]
+    one = jax.ShapeDtypeStruct(whole.shape[1:], whole.dtype)
     return pl.pallas_call(
         finish_kernel,
-        out_shape=like,
-        in_specs=[vmem] * 10,
-        out_specs=[hbm] * 3 + [vmem] * 6,
-        scratch_shapes=[pltpu.SemaphoreType.DMA((3, 2, N))],
+        out_shape=[one] * 3 + [jax.ShapeDtypeStruct(x.shape, x.dtype) for x in like],
+        in_specs=[vmem] * 5,
+        out_specs=[hbm] * 9,
+        scratch_shapes=[pltpu.SemaphoreType.DMA((6 * N + 6,))],
         compiler_params=pltpu.CompilerParams(vmem_limit_bytes=FINISH_LIMIT),
         cost_estimate=pl.CostEstimate(flops=10**8, bytes_accessed=100 * 2**20, transcendentals=0),
         name="finish",
-    )(whole, g_wide, g_tall, factor, *m, *v)
+    )(*moments, whole)
 
 
 def wide_tiles(t, *major):
@@ -571,8 +561,8 @@
             return wide_tiles(one[0]), wide_tiles(one[1]), tall_tiles(one[2])
 
         m, v = moments(m), moments(v)
-        g_wide, g_tall, factor, whole = device_step(g, w, m, v, tiles)
-        new = finish(whole, g_wide, g_tall, factor, m, v)
+        *new_moments, whole = device_step(g, w, m, v, tiles)
+        new = finish(new_moments, whole, (*m, *v))
         shapes = [one.shape for one in arrays[3:]]
         return tuple((from_tall if i % 3 == 2 else from_wide)(one, shape) for i, (one, shape) in enumerate(zip(new, shapes, strict=True)))
 

time: 236 us -> 230 us (0.975)
  Pallas kernels: 236 us -> 230 us
    pallas_call x2, Pallas kernels: 236 us -> 230 us  [the longest x1 213 us: device_step(): pl.pallas_call(step_kernel, out_shape=[pltpu.VMEM((4, tiles, 4, 128), F32...]
where the time goes in v3:
time: 230 us
  Pallas kernels  230 us (100%)
    pallas_call x1, Pallas kernels, device_step(): pl.pallas_call(step_kernel, out_shape=[pltpu.VMEM((4, tiles, 4, 128), F32...  213 us
    pallas_call x1, Pallas kernels, finish(): pl.pallas_call(finish_kernel, out_shape=[one] * 3 + [jax.ShapeDtypeStruct...  16.6 us

profile of v3, /device:TPU:1, one launch (start us, length us, event | category | flops | bytes accessed | tf_op | source)
XLA Modules:
  0.0 230.2 jit_solution(11281617487776096065)
XLA Ops:
  0.6 212.9 %device_step.1 = (f32[4,64,4,128]{3,2,1,0:T(4,128)S(1)}, f32[2,32,8,128]{3,2,1,0:T(8,128)S(1)}, f32[4,64,4,128]{3,2,1,0:T(4,128)S(1)}, f32[2,32,8,128]{3,2,1,0:T...) custom-call(bf16[2,4,4,4,64,8,128]{6,5,4,3,2,1,0:T(8,128)(2,1)} %bitcast.77, bf16[2,4,4,4,64,8,128]{6,5,4,3,2,1,0:T(8,128)(2,1)} %bitcast.78, ...), custom_call_target="tpu_custom_call" | custom-call | tf_op jit(solution)/shard_map/device_step/pallas_call | solution.py:455
  213.6 16.6 %finish.1 = (bf16[2,4,4,4,64,8,128]{6,5,4,3,2,1,0:T(8,128)(2,1)}, bf16[2,4,4,4,64,8,128]{6,5,4,3,2,1,0:T(8,128)(2,1)}, bf16[2,4,4,4,64,8,128]{6,5,4,3,2,1,0:T(8,...) custom-call(f32[4,64,4,128]{3,2,1,0:T(4,128)S(1)} %get-tuple-element, ...), custom_call_target="tpu_custom_call" | custom-call | flops 100000000 | bytes 104857600 | tf_op jit(solution)/shard_map/finish/pallas_call | solution.py:516

commit v4 on v3

--- a/solution.py
+++ b/solution.py
@@ -136,7 +136,7 @@
         for n in range(6):
             own_copy(n, 0, k).start()
 
-    meet([partner] + [device(core, moved(chip, axis, by)) for axis in range(3) for by in range(1, N)])
+    meet([partner] + [device(core, moved(chip, axis, by)) for axis in range(3) for by in (1, N - 1)])
 
     @pl.loop(0, AHEAD)
     def _(k):
@@ -252,20 +252,23 @@
         down.append(third_axis_parts(n, 2))
         third_axis(n, down[n], second_half, 1, 2, s)
     for n in range(6):
+        arrived(blocks(n, (N - 1) * N * N), send1.at[n])
+        arrived(blocks(n, (N - 1) * N), send2.at[n])
+    for n in range(6):
         s = 1 - 2 * COLORS[n][1]
         arrived(r3(n, 0).at[first_half], recv3.at[n, 0])
         third_axis(n, down[n], first_half, 1, 2, s, r3(n, 0).at[first_half])
         arrived(r3(n, 0).at[second_half], recv3.at[n, 1])
         third_axis(n, up[n], second_half, 2, 3, -s, r3(n, 0).at[second_half])
 
-    norm[0] = jnp.zeros(norm.shape[1:], F32)
+    norm[...] = jnp.zeros(norm.shape, F32)
     for n, (which, layer) in enumerate(COLORS):
         ins = third_axis_parts(n, 3)
         for slot in (1, 2):
             arrived(r3(n, slot), recv3.at[n, slot + 1])
             ins.append(r3(n, slot))
 
-        @pl.loop(0, half // step, init_carry=jnp.zeros(norm.shape[1:], F32))
+        @pl.loop(0, half // step, init_carry=jnp.zeros(norm.shape, F32))
         def squares(i, so_far, ins=ins, which=which, layer=layer, n=n):
             at = pl.ds(i * step, step)
             total = ins[0][at].astype(F32)
@@ -281,33 +284,28 @@
                 g_tall[layer, at] = rounded
             return so_far + jnp.sum(total * total, axis=0)
 
-        norm[0] += squares
+        norm[...] += squares
         if which < 2:
             send(g_send.at[n], g_wide.at[n, mine], swap_send, swap_recv, partner)
 
     for n in range(6):
-        arrived(blocks(n, (N - 1) * N * N), send1.at[n])
-        arrived(blocks(n, (N - 1) * N), send2.at[n])
         arrived(blocks(n, N - 1), send3.at[n])
 
-    send(norm.at[0], norm_got.at[0, 0], norm_send.at[0], norm_recv.at[0], partner)
-    arrived(norm_got.at[0, 0], norm_recv.at[0])
-    norm[1] = norm[0] + norm_got[0, 0]
-    for axis in range(3):
-        for d in range(1, N):
-            src, dst = norm.at[1 + axis], norm_got.at[1 + axis, d - 1]
-            send(src, dst, norm_send.at[1], norm_recv.at[1 + axis], device(core, moved(chip, axis, d)))
-        if axis == 0:
-            for i, dst in enumerate((w_chip, w_chip_tall, m_wide, m_tall, v_wide, v_tall)):
-                arrived(dst, load_sem.at[i])
-            arrived(g_wide.at[:, theirs], swap_recv)
-        arrived(norm_got.at[1 + axis], norm_recv.at[1 + axis])
-        total = norm[1 + axis]
-        for d in range(1, N):
-            total = total + norm_got[1 + axis, d - 1]
-        norm[2 + axis] = total
+    me = lax.axis_index("dp")
+    norm_got[me] = jnp.sum(norm[...], axis=0, keepdims=True)
+    apart = DEVICES // N
+    for first in (2 * apart, 3 * apart, apart, 0):
+
+        @pl.loop(max(first, 1), first + apart)
+        def _(d):
+            send(norm_got.at[me], norm_got.at[me], norm_send, norm_recv, {"dp": lax.rem(me + d, DEVICES)})
+
+    for i, dst in enumerate((w_chip, w_chip_tall, m_wide, m_tall, v_wide, v_tall)):
+        arrived(dst, load_sem.at[i])
+    arrived(g_wide.at[:, theirs], swap_recv)
+    arrived(norm_got.at[pl.ds(0, DEVICES - 1)], norm_recv)
     count = 6 * N**3 * 2 * half * 8 * 128
-    everything = jnp.sum(norm[4], keepdims=True)
+    everything = jnp.sum(jnp.sum(norm_got[...], axis=0), keepdims=True)
     factor = jnp.minimum(1.0, 0.5 * lax.rsqrt(everything / count + 1e-30))
 
     def new_weight(old, m, v, grad):
@@ -337,17 +335,21 @@
         along_b(n, here, 0, 0)
         along_a(n, here, 0, 0)
 
+    def new_rows(n, first):
+        at = pl.ds(first, step)
+        old = w_chip[n, at].astype(F32)
+        old = jnp.where(core == 0, old[:, :4], old[:, 4:])
+        scale = jnp.broadcast_to(factor[:, :, None], old.shape)
+        new, m_wide[n, at], v_wide[n, at] = new_weight(old, m_wide[n, at], v_wide[n, at], g_wide[n, at].astype(F32) * scale)
+        return new
+
     for n in range(4):
 
-        @pl.loop(0, 2 * half // step)
+        @pl.loop(0, half // step)
         def _(i, n=n):
-            at = pl.ds(i * step, step)
-            old = w_chip[n, at].astype(F32)
-            old = jnp.where(core == 0, old[:, :4], old[:, 4:])
-            scale = jnp.broadcast_to(factor[:, :, None], old.shape)
-            w_rows[n, at], m_wide[n, at], v_wide[n, at] = new_weight(old, m_wide[n, at], v_wide[n, at], g_wide[n, at].astype(F32) * scale)
-
-        send(w_rows.at[n, theirs], w_got.at[n], back_send, back_recv.at[n], partner)
+            w_rows[n, pl.ds(i * step, step)] = new_rows(n, (1 - core) * half + i * step)
+
+        send(w_rows.at[n], w_got.at[n], back_send, back_recv.at[n], partner)
 
     for n in (4, 5):
         here = at(n, 0, 0, 0)
@@ -368,7 +370,7 @@
         @pl.loop(0, half // step)
         def _(i, n=n, here=here):
             at = pl.ds(i * step, step)
-            kept = w_rows[n, pl.ds(core * half + i * step, step)].astype(F32)
+            kept = new_rows(n, core * half + i * step).astype(F32)
             got = w_got[n, at].astype(F32)
             top, bottom = jnp.where(core == 0, kept, got), jnp.where(core == 0, got, kept)
             here[at] = jnp.concatenate([top, bottom], axis=1).astype(BF16)
@@ -435,8 +437,7 @@
         arrived(blocks(n, N**3), par_send.at[n])
     arrived(g_send, swap_send)
     arrived(w_got, back_send)
-    arrived(norm.at[0], norm_send.at[0])
-    arrived(norm_got.at[pl.ds(1, 3)], norm_send.at[1])
+    arrived(norm_got.at[pl.ds(0, DEVICES - 1)], norm_send)
 
     beyond(N - 1, True)
 
@@ -470,10 +471,10 @@
             pltpu.VMEM((2, half, 8, 128), BF16),
             pltpu.VMEM((4, tiles, 8, 128), BF16),
             pltpu.VMEM((2, half, 8, 128), BF16),
-            pltpu.VMEM((4, tiles, 4, 128), BF16),
             pltpu.VMEM((4, half, 4, 128), BF16),
-            pltpu.VMEM((5, 8, 128), F32),
-            pltpu.VMEM((4, N - 1, 8, 128), F32),
+            pltpu.VMEM((4, half, 4, 128), BF16),
+            pltpu.VMEM((8, 128), F32),
+            pltpu.VMEM((DEVICES, 1, 128), F32),
             dma((AHEAD, 6)),
             dma((6,)),
             dma((6, N)),
@@ -483,8 +484,8 @@
             dma((6, N - 1, N)),
             dma((6,)),
             dma((6, 4)),
-            dma((2,)),
-            dma((4,)),
+            dma,
+            dma,
             dma,
             dma,
             dma,

time: 230 us -> 226 us (0.983)
  Pallas kernels: 230 us -> 225 us
    pallas_call x1, Pallas kernels: 213 us -> 209 us  [device_step(): pl.pallas_call(step_kernel, out_shape=[pltpu.VMEM((4, tiles, 4, 128), F32...]
where the time goes in v4:
time: 226 us
  Pallas kernels  225 us (100%)
    pallas_call x1, Pallas kernels, device_step(): pl.pallas_call(step_kernel, out_shape=[pltpu.VMEM((4, tiles, 4, 128), F32...  209 us
    pallas_call x1, Pallas kernels, finish(): pl.pallas_call(finish_kernel, out_shape=[one] * 3 + [jax.ShapeDtypeStruct...  16.6 us

profile of v4, /device:TPU:1, one launch (start us, length us, event | category | flops | bytes accessed | tf_op | source)
XLA Modules:
  0.0 226.1 jit_solution(17449548786442145565)
XLA Ops:
  0.6 208.8 %device_step.1 = (f32[4,64,4,128]{3,2,1,0:T(4,128)S(1)}, f32[2,32,8,128]{3,2,1,0:T(8,128)S(1)}, f32[4,64,4,128]{3,2,1,0:T(4,128)S(1)}, f32[2,32,8,128]{3,2,1,0:T...) custom-call(bf16[2,4,4,4,64,8,128]{6,5,4,3,2,1,0:T(8,128)(2,1)} %bitcast.77, bf16[2,4,4,4,64,8,128]{6,5,4,3,2,1,0:T(8,128)(2,1)} %bitcast.78, ...), custom_call_target="tpu_custom_call" | custom-call | tf_op jit(solution)/shard_map/device_step/pallas_call | solution.py:456
  209.5 16.6 %finish.1 = (bf16[2,4,4,4,64,8,128]{6,5,4,3,2,1,0:T(8,128)(2,1)}, bf16[2,4,4,4,64,8,128]{6,5,4,3,2,1,0:T(8,128)(2,1)}, bf16[2,4,4,4,64,8,128]{6,5,4,3,2,1,0:T(8,...) custom-call(f32[4,64,4,128]{3,2,1,0:T(4,128)S(1)} %get-tuple-element, ...), custom_call_target="tpu_custom_call" | custom-call | flops 100000000 | bytes 104857600 | tf_op jit(solution)/shard_map/finish/pallas_call | solution.py:517

commit v5 on v4

--- a/solution.py
+++ b/solution.py
@@ -9,7 +9,7 @@
 
 N = 4
 AHEAD = 2
-STEP = 8
+STEP = 32
 STEP_LIMIT, FINISH_LIMIT = 10 * 2**20, 4 * 2**20
 DEVICES = 2 * N**3
 ORDERS = ((0, 1, 2), (1, 2, 0), (2, 0, 1))
@@ -70,6 +70,8 @@
 
 
 def add_up(out, ins, step):
+    step = min(step, out.shape[0])
+
     @pl.loop(0, out.shape[0] // step)
     def _(n):
         at = pl.ds(n * step, step)
@@ -84,7 +86,7 @@
     m_wide, m_tall, v_wide, v_tall, whole,
     own, g_send, g_wide, g_tall, w_chip, w_chip_tall, w_rows, w_got, norm, norm_got,
     own_sem, par_send, par_recv, send1, recv1, send2, recv2, send3, recv3,
-    norm_send, norm_recv, swap_send, swap_recv, back_send, back_recv, load_sem, send_p, recv_p,
+    norm_send, norm_recv, swap_send, swap_recv, back_send, back_recv, load_sem, send_p, recv_p, first_recv,
 ):
     g, w = (g0, g1, g2), (w0, w1, w2)
     core, chip = place()
@@ -138,7 +140,14 @@
 
     meet([partner] + [device(core, moved(chip, axis, by)) for axis in range(3) for by in (1, N - 1)])
 
-    @pl.loop(0, AHEAD)
+    @pl.loop(0, N)
+    def _(q):
+        for n in range(6):
+            a, b, _ = targets(COLORS[n], 0, 0)
+            src = block(g[COLORS[n][0]], COLORS[n], (a, b, q), theirs)
+            send(src, par(n, 0, 0).at[q], par_send.at[n], first_recv.at[n, q], partner)
+
+    @pl.loop(1, AHEAD)
     def _(k):
         for n in range(6):
             push(n, 0, k)
@@ -176,7 +185,21 @@
         send(par(n, t, k), r1(n, t, k), send1.at[n], recv1.at[n, t, k], to(n, 0))
         ask(n, t * N + k + AHEAD)
 
+    for n in range(6):
+        own_copy(n, 0, 0).wait()
+
     @pl.loop(0, N)
+    def _(q):
+        for n in range(6):
+            out = par(n, 0, 0).at[q]
+            arrived(out, first_recv.at[n, q])
+            add_up(out, [own.at[0, n, q], out], step)
+            send(out, r1(n, 0, 0).at[q], send1.at[n], recv1.at[n, 0, 0], to(n, 0))
+
+    for n in range(6):
+        ask(n, AHEAD)
+
+    @pl.loop(1, N)
     def _(k):
         for n in range(6):
             first_axis(n, 0, k, True)
@@ -493,6 +516,7 @@
             dma((6,)),
             dma((6,)),
             dma((6,)),
+            dma((6, N)),
         ],
         compiler_params=pltpu.CompilerParams(collective_id=0, has_side_effects=True, vmem_limit_bytes=STEP_LIMIT),
         name="device_step",

time: 226 us -> 224 us (level)
  no operation moved by 1% of the time
where the time goes in v5:
time: 224 us
  Pallas kernels  224 us (100%)
    pallas_call x1, Pallas kernels, device_step(): pl.pallas_call(step_kernel, out_shape=[pltpu.VMEM((4, tiles, 4, 128), F32...  207 us
    pallas_call x1, Pallas kernels, finish(): pl.pallas_call(finish_kernel, out_shape=[one] * 3 + [jax.ShapeDtypeStruct...  16.6 us

profile of v5, /device:TPU:1, one launch (start us, length us, event | category | flops | bytes accessed | tf_op | source)
XLA Modules:
  0.0 224.3 jit_solution(18183191511225153816)
XLA Ops:
  0.6 207.0 %device_step.1 = (f32[4,64,4,128]{3,2,1,0:T(4,128)S(1)}, f32[2,32,8,128]{3,2,1,0:T(8,128)S(1)}, f32[4,64,4,128]{3,2,1,0:T(4,128)S(1)}, f32[2,32,8,128]{3,2,1,0:T...) custom-call(bf16[2,4,4,4,64,8,128]{6,5,4,3,2,1,0:T(8,128)(2,1)} %bitcast.77, bf16[2,4,4,4,64,8,128]{6,5,4,3,2,1,0:T(8,128)(2,1)} %bitcast.78, ...), custom_call_target="tpu_custom_call" | custom-call | tf_op jit(solution)/shard_map/device_step/pallas_call | solution.py:479
  207.7 16.6 %finish.1 = (bf16[2,4,4,4,64,8,128]{6,5,4,3,2,1,0:T(8,128)(2,1)}, bf16[2,4,4,4,64,8,128]{6,5,4,3,2,1,0:T(8,128)(2,1)}, bf16[2,4,4,4,64,8,128]{6,5,4,3,2,1,0:T(8,...) custom-call(f32[4,64,4,128]{3,2,1,0:T(4,128)S(1)} %get-tuple-element, ...), custom_call_target="tpu_custom_call" | custom-call | flops 100000000 | bytes 104857600 | tf_op jit(solution)/shard_map/finish/pallas_call | solution.py:541
